TPU v7x, 768 devices: a whole 4x8x12 slice. The times are simulated.
768 devices in a mesh: dp: 24 (over y_hi, z), tensor: 32 (over y_lo, x, core).
Axes of the slice: x: 4, y: 8 (y_hi: 2, y_lo: 4; y = y_hi * 4 + y_lo), z: 12, core: 2. Of those that a mesh axis runs over, the one named last changes fastest.
Arguments:
- hidden_slots: bfloat16 [576, 16, 8192], P('dp', None, 'tensor'), may hold values from -6 to 6
- lengths: int32 [24, 24], replicated, may hold values from 1 to 16, 192 in all within a row
- owners: int32 [24, 24], replicated, may hold values from 0 to 23, as said below
- norm_gain: float32 [8192], replicated, may hold values from 0.25 to 1.75
- w_query: bfloat16 [8192, 8192], P(None, 'tensor'), may hold values from -0.0625 to 0.0625
- query_bias: float32 [8192], P('tensor'), may hold values from -3 to 3
- w_keyvalue: bfloat16 [8192, 2048], P('tensor'), may hold values from -0.0625 to 0.0625
- keyvalue_bias: float32 [2048], replicated, may hold values from -3 to 3
- grad_attention: bfloat16 [4608, 8192], P('dp', 'tensor'), may hold values from -6 to 6
Outputs:
- attention: bfloat16 [4608, 8192], P('dp', 'tensor')
- input_grad: bfloat16 [4608, 8192], P('dp', 'tensor')
Inputs may be any that keep to these rules, and one draw needn't show every extreme that they name: `owners`: every owner appears exactly once in each row and exactly once in each column j, so each micro-batch takes one rollout from every owner and each owner holds exactly one rollout in each of its 24 slots. `lengths`: each row sums to 192, and its largest entry is 16.
All inputs are finite; a program needn't handle non-finite values.
Results may differ from a plain program's by a relative error of at most 0.013.
Values may be sent and summed in bfloat16 or wider, within the bound.
A program may use at most 64 MiB of HBM per device.

v0:
```python
import jax
import jax.numpy as jnp
from jax import lax
from jax.sharding import PartitionSpec as P

D = 8192
HEADS = 64
KV_HEADS = 8
HEAD_DIM = 128


EPSILON = 1e-06
ROPE_BASE = 1000000.0


def filled_up(lines, size):
    spare = -len(lines) % size
    return jnp.pad(lines, [(0, spare)] + [(0, 0)] * (lines.ndim - 1))


def total_of(shard, axis):
    lines = shard.reshape(-1, *shard.shape[1:][-1:])
    own = lax.psum_scatter(
        filled_up(lines, lax.axis_size(axis)), axis, scatter_dimension=0, tiled=True
    )
    whole = lax.all_gather(own, axis).reshape(-1, *lines.shape[1:])
    return lax.slice_in_dim(whole, 0, len(lines)).reshape(shard.shape)


def cut_along(shard, dim, size):
    before, after = (shard.shape[:dim], shard.shape[dim + 1 :])
    return jnp.moveaxis(shard.reshape(*before, size, -1, *after), dim, 0)


def sum_at_owner(shard, axis, dim):
    tiles = cut_along(shard, dim, lax.axis_size(axis))
    arrived = lax.all_to_all(tiles, axis, split_axis=0, concat_axis=0, tiled=True)
    return arrived.sum(axis=0)


def from_everyone(shard, axis):
    copies = jnp.broadcast_to(shard, (lax.axis_size(axis), *shard.shape))
    return lax.all_to_all(copies, axis, split_axis=0, concat_axis=0, tiled=True)


def joined_along(tiles, dim):
    tiles = jnp.moveaxis(tiles, 0, dim)
    dims = tiles.shape
    return tiles.reshape(*dims[:dim], dims[dim] * dims[dim + 1], *dims[dim + 2 :])


def collect(shard, axis, dim):
    tiles = from_everyone(shard, axis)
    return joined_along(tiles, dim)


def taken_together(shard, axis):
    everything = from_everyone(shard, axis)
    return jnp.sum(everything, axis=0)


def packing(length_row, row_count):
    starts = jnp.cumsum(length_row) - length_row
    places = jnp.arange(row_count, dtype=jnp.int32)
    segment = jnp.sum((places[:, None] >= starts[None, 1:]).astype(jnp.int32), axis=1)
    onehot = (segment[:, None] == jnp.arange(length_row.shape[0], dtype=jnp.int32)[None, :]).astype(
        jnp.int32
    )
    offset = places - jnp.sum(onehot * starts[None, :], axis=1)
    return (segment, offset, onehot)


def tables(offset, head_width):
    halfway = head_width // 2
    frequency = ROPE_BASE ** (-2.0 * jnp.arange(halfway, dtype=jnp.float32) / head_width)
    angles = offset.astype(jnp.float32)[:, None] * frequency[None, :]
    angles = jnp.concatenate([angles, angles], axis=1)
    return (jnp.cos(angles)[:, None, :], jnp.sin(angles)[:, None, :])


def rotate(values, cosine, sine_table):
    halfway = values.shape[-1] // 2
    turned = jnp.concatenate([-values[..., halfway:], values[..., :halfway]], axis=-1)
    return values * cosine + turned * sine_table


def unrotate(gradient, cosine, sine_table):
    halfway = gradient.shape[-1] // 2
    scaled = gradient * sine_table
    turned = jnp.concatenate([scaled[..., halfway:], -scaled[..., :halfway]], axis=-1)
    return gradient * cosine + turned


def normalize(hidden, norm_gain):
    widened = hidden.astype(jnp.float32)
    inverse = lax.rsqrt(jnp.mean(widened * widened, axis=1) + EPSILON)
    normed = (widened * inverse[:, None] * norm_gain).astype(jnp.bfloat16)
    return (widened, inverse, normed)


def masked_softmax(scores, allowed):
    scores = jnp.where(allowed, scores, -1e30)
    highest = jnp.max(scores, axis=-1, keepdims=True)
    exponent = jnp.where(allowed, jnp.exp(scores - highest), 0.0)
    return exponent / jnp.sum(exponent, axis=-1, keepdims=True)


def contract_last(operand, weights):
    return lax.dot_general(
        operand, weights, (((1,), (1,)), ((), ())), preferred_element_type=jnp.float32
    )


def on_device(
    hidden_slots,
    lengths,
    owners,
    norm_gain,
    w_query,
    query_bias,
    w_keyvalue,
    keyvalue_bias,
    grad_attention,
):
    slot_count, window, feature_part = hidden_slots.shape
    owner_count = lax.axis_size("dp")
    dp_index = lax.axis_index("dp")
    picked = (owners == dp_index).astype(jnp.bfloat16)
    outgoing = jnp.einsum(
        "bj,jld->bld", picked, hidden_slots, preferred_element_type=jnp.float32
    ).astype(jnp.bfloat16)
    arrived = lax.all_to_all(outgoing, "dp", split_axis=0, concat_axis=0, tiled=True)
    row_count = grad_attention.shape[0]
    length_row = lax.dynamic_index_in_dim(lengths, dp_index, 0, keepdims=False)
    owner_row = lax.dynamic_index_in_dim(owners, dp_index, 0, keepdims=False)
    segment, offset, onehot = packing(length_row, row_count)
    source = jnp.sum(onehot * owner_row[None, :], axis=1)
    row_index = source * window + offset
    local_rows = jnp.take(arrived.reshape(owner_count * window, feature_part), row_index, axis=0)
    full_rows = lax.all_gather(local_rows, "tensor", axis=1, tiled=True)
    widened, inverse, normed = normalize(full_rows, norm_gain)
    tensor_index = lax.axis_index("tensor")
    lane_count = lax.axis_size("tensor")
    column_start = tensor_index * feature_part
    normed_local = lax.dynamic_slice_in_dim(normed, column_start, feature_part, 1)
    query_full = jnp.dot(normed, w_query, preferred_element_type=jnp.float32) + query_bias
    partial_kv = jnp.dot(normed_local, w_keyvalue, preferred_element_type=jnp.float32)
    keyvalue = total_of(partial_kv, "tensor") + keyvalue_bias
    local_heads = w_query.shape[1] // HEAD_DIM
    kv_width = KV_HEADS * HEAD_DIM
    half_dim = HEAD_DIM // 2
    score_scale = HEAD_DIM ** (-0.5)
    group_index = tensor_index * local_heads // (HEADS // KV_HEADS)
    key_start = group_index * HEAD_DIM
    cosine, sine_table = tables(offset, HEAD_DIM)
    query_rot = rotate(
        query_full.reshape(row_count, local_heads, HEAD_DIM), cosine, sine_table
    ).astype(jnp.bfloat16)
    key_rot = rotate(
        lax.dynamic_slice_in_dim(keyvalue, key_start, HEAD_DIM, 1), cosine[:, 0], sine_table[:, 0]
    ).astype(jnp.bfloat16)
    value_one = lax.dynamic_slice_in_dim(keyvalue, kv_width + key_start, HEAD_DIM, 1).astype(
        jnp.bfloat16
    )
    places = jnp.arange(row_count, dtype=jnp.int32)
    allowed = (segment[:, None] == segment[None, :]) & (places[None, :] <= places[:, None])
    scores = (
        jnp.einsum("qhd,kd->hqk", query_rot, key_rot, preferred_element_type=jnp.float32)
        * score_scale
    )
    attn_weights = masked_softmax(scores, allowed[None])
    low_weights = attn_weights.astype(jnp.bfloat16)
    attended = jnp.einsum(
        "hqk,kd->qhd", low_weights, value_one, preferred_element_type=jnp.float32
    ).astype(jnp.bfloat16)
    upstream = grad_attention.reshape(row_count, local_heads, HEAD_DIM)
    weight_grad = jnp.einsum("qhd,kd->hqk", upstream, value_one, preferred_element_type=jnp.float32)
    value_grad = jnp.einsum(
        "hqk,qhd->kd", low_weights, upstream, preferred_element_type=jnp.float32
    )
    row_inner = jnp.sum(attn_weights * weight_grad, axis=-1, keepdims=True)
    score_grad = (attn_weights * (weight_grad - row_inner) * score_scale).astype(jnp.bfloat16)
    query_grad = unrotate(
        jnp.einsum("hqk,kd->qhd", score_grad, key_rot, preferred_element_type=jnp.float32),
        cosine,
        sine_table,
    ).astype(jnp.bfloat16)
    key_grad = jnp.einsum("hqk,qhd->kd", score_grad, query_rot, preferred_element_type=jnp.float32)
    zeros_kv = jnp.zeros((row_count, 2 * kv_width), jnp.float32)
    partial_grad = lax.dynamic_update_slice_in_dim(zeros_kv, key_grad, key_start, 1)
    partial_grad = lax.dynamic_update_slice_in_dim(
        partial_grad, value_grad, kv_width + key_start, 1
    )
    paired = (
        partial_grad.reshape(row_count, 2, KV_HEADS, 2, half_dim)
        .transpose(0, 1, 2, 4, 3)
        .reshape(row_count, 2 * kv_width)
    )
    share_width = 2 * kv_width // lane_count
    shared = sum_at_owner(paired, "tensor", 1)
    position = tensor_index * share_width + jnp.arange(share_width // 2, dtype=jnp.int32) * 2
    frequency_index = position // 2 % half_dim
    is_key = (position < kv_width).astype(jnp.float32)
    frequency = ROPE_BASE ** (-2.0 * frequency_index.astype(jnp.float32) / HEAD_DIM)
    angles = offset.astype(jnp.float32)[:, None] * frequency[None, :]
    cos_pair = is_key[None, :] * jnp.cos(angles) + (1.0 - is_key[None, :])
    sin_pair = is_key[None, :] * jnp.sin(angles)
    pairs = shared.reshape(row_count, share_width // 2, 2)
    first_half = pairs[:, :, 0] * cos_pair + pairs[:, :, 1] * sin_pair
    second_half = pairs[:, :, 1] * cos_pair - pairs[:, :, 0] * sin_pair
    finished = (
        jnp.stack([first_half, second_half], axis=2)
        .reshape(row_count, share_width)
        .astype(jnp.bfloat16)
    )
    gathered = collect(finished, "tensor", 1)
    kv_grad = (
        gathered.reshape(row_count, 2, KV_HEADS, half_dim, 2)
        .transpose(0, 1, 2, 4, 3)
        .reshape(row_count, 2 * kv_width)
    )
    query_flat = query_grad.reshape(row_count, local_heads * HEAD_DIM)
    query_part = contract_last(query_flat, w_query)
    normed_grad = lax.psum_scatter(
        query_part.astype(jnp.bfloat16), "tensor", scatter_dimension=1, tiled=True
    ).astype(jnp.float32) + contract_last(kv_grad, w_keyvalue)
    gain_local = lax.dynamic_slice_in_dim(norm_gain, column_start, feature_part, 0)
    hidden_local = local_rows.astype(jnp.float32)
    scaled = gain_local * normed_grad
    row_stat = taken_together(jnp.sum(scaled * hidden_local, axis=1), "tensor") / D
    input_grad = (
        inverse[:, None] * scaled - hidden_local * (inverse**3 * row_stat)[:, None]
    ).astype(jnp.bfloat16)
    return (attended.reshape(row_count, local_heads * HEAD_DIM), input_grad)


def solution(mesh):
    in_specs = (
        P("dp", None, "tensor"),
        P(),
        P(),
        P(),
        P(None, "tensor"),
        P("tensor"),
        P("tensor", None),
        P(),
        P("dp", "tensor"),
    )
    out_specs = (P("dp", "tensor"), P("dp", "tensor"))
    return jax.shard_map(
        on_device, mesh=mesh, in_specs=in_specs, out_specs=out_specs, check_vma=False
    )
```

profile of v0, /device:TPU:1, one launch (start us, length us, event | category | flops | bytes accessed | tf_op | source)
XLA Modules:
  0.0 484.1 jit_solution(8507905309290204347)
XLA Ops:
  7.2 1.2 convolution_convert_fusion.1
  8.4 0.7 copy.87
  9.2 21.2 %all-to-all-start = ((bf16[24,16,256]{2,1,0:T(8,128)(2,1)}), bf16[24,16,256]{2,1,0:T(8,128)(2,1)S(1)}, u32[]{:S(2)}, u32[]{:S(2)}) async-start(bf16[24,16,256]{2,1,0:T(8,128)(2,1)} %copy.87), calls=%async_computation | async-start | bytes 393216 | tf_op jit(solution)/shard_map/all_to_all | solution.py:132
  30.4 0.7 fusion.85
  31.3 0.7 bitcast_subtract_fusion.1
  32.0 0.7 fusion.76
  33.1 13.2 %all-to-all-done = bf16[24,16,256]{2,1,0:T(8,128)(2,1)S(1)} async-done(((bf16[24,16,256]{2,1,0:T(8,128)(2,1)}), bf16[24,16,256]{2,1,0:T(8,128)(2,1)S(1)}, u32[]{:S(2)}, u32[]{:S(2)}) %all-to-all-start) | async-done | bytes 196640 | tf_op jit(solution)/shard_map/all_to_all | solution.py:132
  46.3 1.0 gather_fusion
  47.3 0.7 broadcast_select_fusion
  48.1 66.3 %all-gather.5.cloned.1.call-done = bf16[192,8192]{1,0:T(8,128)(2,1)} async-done(((bf16[192,256]{1,0:T(8,128)(2,1)}), bf16[192,8192]{1,0:T(8,128)(2,1)}) %all-gather.5.cloned.1.call-update) | async-done | bytes 3145744 | tf_op jit(solution)/shard_map/all_gather | solution.py:140
  114.3 2.8 fusion.3
  117.2 0.9 fusion.5
  118.0 1.7 copy-done.1
  120.1 78.2 %fusion = f32[8,2048]{1,0:T(8,128)S(1)} fusion(f32[192,2048]{1,0:T(8,128)S(1)} %fusion.43), kind=kCustom, calls=%all-reduce-scatter | all-reduce-scatter fusion | flops 524289 | bytes 1642496
  198.3 1.3 collective-permute-start.6
  199.6 1.3 collective-permute-start.5
  200.9 1.3 collective-permute-start.7
  202.2 1.3 collective-permute-start.4
  203.5 11.7 %collective-permute-start.3 = (f32[8,2048]{1,0:T(8,128)S(1)}, f32[8,2048]{1,0:T(8,128)S(1)}, u32[]{:S(2)}, u32[]{:S(2)}) collective-permute-start(f32[8,2048]{1,0:T(8,128)S(1)} %fusion), channel_id=1, source_target_pairs={{0,4},{1,5},{2,6},{3,7},{4,8},{5,9},{6,10},{7,11},{8,12},{9,13},{1... | collective-permute-start | bytes 196616
  215.3 1.3 collective-permute-start.2
  216.6 4.0 collective-permute-start.1
  220.6 2.2 collective-permute-start
  222.8 1.3 dynamic-slice.6
  224.8 1.0 concatenate.24
  226.6 0.7 fusion.33
  227.4 4.1 fusion.16
  231.7 60.7 %all-gather.7.cloned.1.call-done = f32[32,6,2048]{2,1,0:T(8,128)} async-done(((f32[1,6,2048]{2,1,0:T(8,128)}), f32[32,6,2048]{2,1,0:T(8,128)}) %all-gather.7.cloned.1.call-update) | async-done | bytes 1572880 | tf_op jit(solution)/shard_map/all_gather | solution.py:26
  292.5 1.6 reshape.447
  294.7 0.8 copy-done.3
  296.1 1.2 fusion.88
  297.8 5.4 %convolution_convert_fusion = bf16[192,8192]{1,0:T(8,128)(2,1)} fusion(bf16[8192,256]{1,0:T(8,128)(2,1)} %param.13, f32[192,2,64]{2,0,1:T(8,128)S(1)} %get-tuple-element.7, f32[192,2,64]{2,0,1:T(8,128)S(1)} %get-tuple-element.6, f32[192,2,128]{2,0,1:T(8,128)S(1)} %get-tuple-element.20, f32[192,128]{1,0:T(8,128)S(1)} %get-tuple-element.10), kind=kOutput, calls=%fused_computation.3 | convolution fusion | flops 807075840 | bytes 7831552 | tf_op jit(solution)/shard_map/dot_general | solution.py:109
  303.4 1.6 fusion.18
  305.0 1.4 fusion.17
  306.4 3.0 copy.99
  309.4 3.7 reshape_reshape.6
  313.1 5.7 %all-to-all-start.1 = ((f32[32,192,64]{1,2,0:T(8,128)}), f32[32,192,64]{1,2,0:T(8,128)S(1)}, u32[]{:S(2)}, u32[]{:S(2)}) async-start(f32[32,192,64]{1,2,0:T(8,128)} %bitcast.121), calls=%async_computation.2 | async-start | bytes 4194304 | tf_op jit(solution)/shard_map/all_to_all | solution.py:37
  318.9 54.4 %all-to-all-done.1 = f32[32,192,64]{1,2,0:T(8,128)S(1)} async-done(((f32[32,192,64]{1,2,0:T(8,128)}), f32[32,192,64]{1,2,0:T(8,128)S(1)}, u32[]{:S(2)}, u32[]{:S(2)}) %all-to-all-start.1) | async-done | bytes 1572896 | tf_op jit(solution)/shard_map/all_to_all | solution.py:37
  373.8 1.1 broadcast_in_dim.40
  374.9 5.2 %all-to-all-start.2 = ((bf16[32,192,64]{1,2,0:T(8,128)(2,1)}), bf16[32,192,64]{1,2,0:T(8,128)(2,1)S(1)}, u32[]{:S(2)}, u32[]{:S(2)}) async-start(bf16[32,192,64]{1,2,0:T(8,128)(2,1)} %broadcast_in_dim.40), calls=%async_computation.3 | async-start | bytes 2097152 | tf_op jit(solution)/shard_map/all_to_all | solution.py:43
  380.1 0.8 dynamic_slice.24
  380.8 28.1 %all-to-all-done.2 = bf16[32,192,64]{1,2,0:T(8,128)(2,1)S(1)} async-done(((bf16[32,192,64]{1,2,0:T(8,128)(2,1)}), bf16[32,192,64]{1,2,0:T(8,128)(2,1)S(1)}, u32[]{:S(2)}, u32[]{:S(2)}) %all-to-all-start.2) | async-done | bytes 786464 | tf_op jit(solution)/shard_map/all_to_all | solution.py:43
  409.7 49.2 %reduce-scatter.4.cloned.1.call-done = bf16[192,256]{1,0:T(8,128)(2,1)} async-done(((bf16[192,8192]{1,0:T(8,128)(2,1)}), bf16[192,256]{1,0:T(8,128)(2,1)}) %reduce-scatter.4.cloned.1.call-update) | async-done | bytes 98320 | tf_op jit(solution)/shard_map/reduce_scatter | solution.py:224
  458.9 1.5 fusion.24
  461.0 7.9 %all-to-all-start.3 = ((f32[32,1,192]{2,1,0:T(1,128)}), f32[32,1,192]{2,1,0:T(1,128)S(1)}, u32[]{:S(2)}, u32[]{:S(2)}) async-start(f32[32,1,192]{2,1,0:T(1,128)} %broadcast_in_dim.41), calls=%async_computation.4 | async-start | bytes 65536 | tf_op jit(solution)/shard_map/all_to_all | solution.py:43
  468.9 1.5 fusion.19
  470.4 0.7 copy.141
  471.0 5.6 %all-to-all-done.3 = f32[32,1,192]{2,1,0:T(1,128)S(1)} async-done(((f32[32,1,192]{2,1,0:T(1,128)}), f32[32,1,192]{2,1,0:T(1,128)S(1)}, u32[]{:S(2)}, u32[]{:S(2)}) %all-to-all-start.3) | async-done | bytes 24608 | tf_op jit(solution)/shard_map/all_to_all | solution.py:43
  476.7 0.8 fusion.26
  (77 shorter events, 5.8 us)
Async XLA Ops:
  7.2 112.5 %copy-start = (bf16[256,2048]{1,0:T(8,128)(2,1)S(1)}, bf16[256,2048]{1,0:T(8,128)(2,1)}, u32[]{:S(2)}) copy-start(bf16[256,2048]{1,0:T(8,128)(2,1)} %param.15) | copy-start | bytes 3145732
  7.2 109.9 %copy-start.8 = (f32[8192]{0:T(1024)S(1)}, f32[8192]{0:T(1024)}, u32[]{:S(2)}) copy-start(f32[8192]{0:T(1024)} %param.12) | copy-start | bytes 98308
  9.2 37.1 %all-to-all-start = ((bf16[24,16,256]{2,1,0:T(8,128)(2,1)}), bf16[24,16,256]{2,1,0:T(8,128)(2,1)S(1)}, u32[]{:S(2)}, u32[]{:S(2)}) async-start(bf16[24,16,256]{2,1,0:T(8,128)(2,1)} %copy.87), calls=%async_computation | async-start | bytes 393216 | tf_op jit(solution)/shard_map/all_to_all | solution.py:132
  30.3 84.0 %all-gather.5.cloned.1.call-start = ((), (), s32[]{:S(2)}) async-start(), calls=%async_computation.5 | async-start | bytes 3244032 | tf_op jit(solution)/shard_map/all_gather | solution.py:140
  48.0 244.5 %all-gather.7.cloned.1.call-start = ((), (), s32[]{:S(2)}) async-start(), calls=%async_computation.7 | async-start | bytes 2162688 | tf_op jit(solution)/shard_map/all_gather | solution.py:26
  114.3 2.8 copy-start.2
  118.0 1.7 copy-start.1
  119.7 107.7 %copy-start.10 = (f32[256]{0:T(256)S(1)}, f32[256]{0:T(256)}, u32[]{:S(2)}) copy-start(f32[256]{0:T(256)} %param.14) | copy-start | bytes 3076
  198.3 18.3 %collective-permute-start.6 = (f32[8,2048]{1,0:T(8,128)S(1)}, f32[8,2048]{1,0:T(8,128)S(1)}, u32[]{:S(2)}, u32[]{:S(2)}) collective-permute-start(f32[8,2048]{1,0:T(8,128)S(1)} %fusion), channel_id=1, source_target_pairs={{0,7},{1,8},{2,9},{3,10},{4,11},{5,12},{6,13},{7,14},{8,15},{9,16}... | collective-permute-start | bytes 196616
  199.6 21.0 %collective-permute-start.5 = (f32[8,2048]{1,0:T(8,128)S(1)}, f32[8,2048]{1,0:T(8,128)S(1)}, u32[]{:S(2)}, u32[]{:S(2)}) collective-permute-start(f32[8,2048]{1,0:T(8,128)S(1)} %fusion), channel_id=1, source_target_pairs={{0,6},{1,7},{2,8},{3,9},{4,10},{5,11},{6,12},{7,13},{8,14},{9,15},... | collective-permute-start | bytes 196616
  200.9 14.3 %collective-permute-start.7 = (f32[6,2048]{1,0:T(8,128)S(1)}, f32[6,2048]{1,0:T(8,128)S(1)}, u32[]{:S(2)}, u32[]{:S(2)}) collective-permute-start(f32[6,2048]{1,0:T(8,128)S(1)} %slice.46), channel_id=1, source_target_pairs={{0,8},{1,9},{2,10},{3,11},{4,12},{5,13},{6,14},{7,15},{8,16},{9,17... | collective-permute-start | bytes 147464
  202.2 22.5 %collective-permute-start.4 = (f32[8,2048]{1,0:T(8,128)S(1)}, f32[8,2048]{1,0:T(8,128)S(1)}, u32[]{:S(2)}, u32[]{:S(2)}) collective-permute-start(f32[8,2048]{1,0:T(8,128)S(1)} %fusion), channel_id=1, source_target_pairs={{0,5},{1,6},{2,7},{3,8},{4,9},{5,10},{6,11},{7,12},{8,13},{9,14},{... | collective-permute-start | bytes 196616
  203.5 21.2 %collective-permute-start.3 = (f32[8,2048]{1,0:T(8,128)S(1)}, f32[8,2048]{1,0:T(8,128)S(1)}, u32[]{:S(2)}, u32[]{:S(2)}) collective-permute-start(f32[8,2048]{1,0:T(8,128)S(1)} %fusion), channel_id=1, source_target_pairs={{0,4},{1,5},{2,6},{3,7},{4,8},{5,9},{6,10},{7,11},{8,12},{9,13},{1... | collective-permute-start | bytes 196616
  215.3 9.5 %collective-permute-start.2 = (f32[8,2048]{1,0:T(8,128)S(1)}, f32[8,2048]{1,0:T(8,128)S(1)}, u32[]{:S(2)}, u32[]{:S(2)}) collective-permute-start(f32[8,2048]{1,0:T(8,128)S(1)} %fusion), channel_id=1, source_target_pairs={{0,3},{1,4},{2,5},{3,6},{4,7},{5,8},{6,9},{7,10},{8,11},{9,12},{10... | collective-permute-start | bytes 196616
  216.6 8.2 %collective-permute-start.1 = (f32[8,2048]{1,0:T(8,128)S(1)}, f32[8,2048]{1,0:T(8,128)S(1)}, u32[]{:S(2)}, u32[]{:S(2)}) collective-permute-start(f32[8,2048]{1,0:T(8,128)S(1)} %fusion), channel_id=1, source_target_pairs={{0,2},{1,3},{2,4},{3,5},{4,6},{5,7},{6,8},{7,9},{8,10},{9,11},{10,... | collective-permute-start | bytes 196616
  220.6 4.2 collective-permute-start
  226.5 232.4 %reduce-scatter.4.cloned.1.call-start = ((), (), s32[]{:S(2)}) async-start(), calls=%async_computation.6 | async-start | bytes 3244032 | tf_op jit(solution)/shard_map/reduce_scatter | solution.py:224
  231.6 62.6 %copy-start.9 = (f32[2048]{0:T(1024)S(1)}, f32[2048]{0:T(1024)}, u32[]{:S(2)}) copy-start(f32[2048]{0:T(1024)} %param.16) | copy-start | bytes 24580
  231.7 62.7 %copy-start.6 = (bf16[192,256]{1,0:T(8,128)(2,1)S(1)}, bf16[192,256]{1,0:T(8,128)(2,1)}, u32[]{:S(2)}) copy-start(bf16[192,256]{1,0:T(8,128)(2,1)} %param.17) | copy-start | bytes 294916
  294.3 1.2 copy-start.3
  294.7 3.0 copy-start.5
  296.0 7.2 %copy-start.7 = (bf16[192,128,1]{1,0,2:T(8,128)(2,1)}, bf16[192,128,1]{1,0,2:T(8,128)(2,1)S(1)}, u32[]{:S(2)}) copy-start(bf16[192,128,1]{1,0,2:T(8,128)(2,1)S(1)} %get-tuple-element.11) | copy-start | bytes 147460
  297.3 5.9 %copy-start.11 = (f32[2,192,192]{1,2,0:T(8,128)}, f32[2,192,192]{1,2,0:T(8,128)S(1)}, u32[]{:S(2)}) copy-start(f32[2,192,192]{1,2,0:T(8,128)S(1)} %get-tuple-element.18) | copy-start | bytes 884740
  313.1 60.1 %all-to-all-start.1 = ((f32[32,192,64]{1,2,0:T(8,128)}), f32[32,192,64]{1,2,0:T(8,128)S(1)}, u32[]{:S(2)}, u32[]{:S(2)}) async-start(f32[32,192,64]{1,2,0:T(8,128)} %bitcast.121), calls=%async_computation.2 | async-start | bytes 4194304 | tf_op jit(solution)/shard_map/all_to_all | solution.py:37
  374.9 84.0 %copy-start.4 = (bf16[192,256]{1,0:T(8,128)(2,1)S(1)}, bf16[192,256]{1,0:T(8,128)(2,1)}, u32[]{:S(2)}) copy-start(bf16[192,256]{1,0:T(8,128)(2,1)} %broadcast_select_fusion) | copy-start | bytes 294916
  374.9 34.0 %all-to-all-start.2 = ((bf16[32,192,64]{1,2,0:T(8,128)(2,1)}), bf16[32,192,64]{1,2,0:T(8,128)(2,1)S(1)}, u32[]{:S(2)}, u32[]{:S(2)}) async-start(bf16[32,192,64]{1,2,0:T(8,128)(2,1)} %broadcast_in_dim.40), calls=%async_computation.3 | async-start | bytes 2097152 | tf_op jit(solution)/shard_map/all_to_all | solution.py:43
  461.0 15.6 %all-to-all-start.3 = ((f32[32,1,192]{2,1,0:T(1,128)}), f32[32,1,192]{2,1,0:T(1,128)S(1)}, u32[]{:S(2)}, u32[]{:S(2)}) async-start(f32[32,1,192]{2,1,0:T(1,128)} %broadcast_in_dim.41), calls=%async_computation.4 | async-start | bytes 65536 | tf_op jit(solution)/shard_map/all_to_all | solution.py:43
Sparse Core Ops, SparseCore 0:
  48.1 66.1 all-gather.4
  226.6 65.8 all-gather.6
  303.4 155.4 reduce-scatter.3
where the time goes:
time: 485 us; the launch traced here: 484 us
  waiting for transfers between devices  278 us (57%)
  blocking collectives  78.2 us (16%)
  starting transfers between devices  64.5 us (13%)
  local copies, waits for them, and re-layouts  20.7 us (4%)
  matrix products  18.9 us (4%)
  between operations  15 us (3%)
  other arithmetic  9.29 us (2%)
    unnamed x1, blocking collectives  78.2 us
    all_gather x1, waiting for transfers between devices, on_device(): full_rows = lax.all_gather(local_rows, 'tensor', axis=1, tiled=True)  66.3 us
    all_gather x1, waiting for transfers between devices, total_of(): whole = lax.all_gather(own, axis).reshape(-1, *lines.shape[1:])  60.7 us
    all_to_all x1, waiting for transfers between devices, sum_at_owner(): lax.all_to_all(tiles, axis, split_axis=0, concat_axis=0, tiled=True)  54.4 us
    reduce_scatter x1, waiting for transfers between devices, on_device(): lax.psum_scatter(query_part.astype(jnp.bfloat16), 'tensor', scatter_dimen...  49.2 us
    all_to_all x2, waiting for transfers between devices, from_everyone(): return lax.all_to_all(copies, axis, split_axis=0, concat_axis=0, tiled=True)  33.7 us
    unnamed x8, starting transfers between devices  24.4 us
    all_to_all x1, starting transfers between devices, on_device(): lax.all_to_all(outgoing, 'dp', split_axis=0, concat_axis=0, tiled=True)  21.2 us
  transfers between devices with their start and end apart: 15, of which 7 were waited for; matrix products, arithmetic and copies ran while one was open for 5% of the time, Pallas kernels for 0%

commit v1 on v0

v1 whole, which is shorter than its diff:
```python
import jax
import jax.numpy as jnp
import numpy as np
from jax import lax
from jax.experimental import pallas as pl
from jax.experimental.pallas import tpu as pltpu
from jax.sharding import PartitionSpec as P

D = 8192
HEADS = 64
KV_HEADS = 8
HEAD_DIM = 128
EPSILON = 1e-06
ROPE_BASE = 1000000.0
N_DP = 24
WINDOW = 16
ROWS = 192
HALF = 96
PART = 256
LANES = 32
HALF_DIM = HEAD_DIM // 2
SCALE = HEAD_DIM ** (-0.5)
MESH = pl.DeviceIdType.MESH
F32 = jnp.float32
BF16 = jnp.bfloat16
TREE_SLOTS = 35
GRAD_ROWS = HALF + 16
ORDER = (1, 2, 3, 0)


def mm(a, b):
    return jnp.dot(a, b, preferred_element_type=F32)


def mm_nt(a, b):
    return lax.dot_general(a, b, (((1,), (1,)), ((), ())), preferred_element_type=F32)


def mm_tn(a, b):
    return lax.dot_general(a, b, (((0,), (0,)), ((), ())), preferred_element_type=F32)


def exact_nt(a, b):
    return lax.dot_general(
        a, b, (((1,), (1,)), ((), ())), preferred_element_type=F32, precision=lax.Precision.HIGHEST
    )


def exact_mm(a, b):
    return lax.dot_general(
        a, b, (((1,), (0,)), ((), ())), preferred_element_type=F32, precision=lax.Precision.HIGHEST
    )


def iota(shape, dim):
    return lax.broadcasted_iota(jnp.int32, shape, dim)


class Links:
    def __init__(self, dp):
        self.dp = dp
        self.sent = []

    def copy(self, src, dst, send_sem, recv_sem, peer):
        return pltpu.make_async_remote_copy(
            src_ref=src,
            dst_ref=dst,
            send_sem=send_sem,
            recv_sem=recv_sem,
            device_id=(self.dp, peer),
            device_id_type=MESH,
        )

    def send(self, src, dst, send_sem, recv_sem, peer):
        one = self.copy(src, dst, send_sem, recv_sem, peer)
        one.start()
        self.sent.append(one)

    def wait(self, dst, send_sem, recv_sem, peer):
        self.copy(dst, dst, send_sem, recv_sem, peer).wait_recv()

    def drain(self):
        for one in self.sent:
            one.wait_send()


class Tree:
    def __init__(self, links, place, buffer, split, send_sems, recv_sems):
        self.links = links
        self.place = place
        self.buffer = buffer
        self.split = split
        self.ss = send_sems
        self.rs = recv_sems

    def block(self, tid):
        return self.buffer.at[tid]

    def part(self, tid, which):
        size = self.buffer.shape[1]
        if which == 0:
            return self.buffer.at[tid, pl.ds(0, self.split)]
        return self.buffer.at[tid, pl.ds(self.split, size - self.split)]

    def send(self, slot, ref, peer):
        self.links.send(ref, ref, self.ss.at[slot], self.rs.at[slot], peer)

    def wait(self, slot, ref, peer):
        self.links.wait(ref, self.ss.at[slot], self.rs.at[slot], peer)

    def spread(self, k):
        p = self.place
        ref = self.block(p.tid(p.ysrc(k), p.x, p.c))
        self.send(3 + k, ref, p.right)
        self.send(7 + k, ref, p.left)
        self.send(19 + k, ref, p.partner)

    def start(self):
        p = self.place
        ref = self.block(p.t)
        for k in (1, 2, 3):
            self.send(k - 1, ref, p.tid(p.ydst(k), p.x, p.c))
        self.spread(0)

    def step_y(self, k):
        p = self.place
        self.wait(k - 1, self.block(p.tid(p.ysrc(k), p.x, p.c)), p.tid(p.ysrc(k), p.x, p.c))
        self.spread(k)

    def step_x(self, k):
        p = self.place
        tid = p.tid(p.ysrc(k), p.xat(3), p.c)
        self.wait(3 + k, self.block(tid), p.left)
        self.send(11 + k, self.part(tid, 0), p.right)
        self.send(23 + k, self.block(tid), p.partner)
        tid = p.tid(p.ysrc(k), p.xat(1), p.c)
        self.wait(7 + k, self.block(tid), p.right)
        self.send(15 + k, self.part(tid, 1), p.left)
        self.send(27 + k, self.block(tid), p.partner)

    def step_far(self, k):
        p = self.place
        tid = p.tid(p.ysrc(k), p.xat(2), p.c)
        self.wait(11 + k, self.part(tid, 0), p.left)
        self.wait(15 + k, self.part(tid, 1), p.right)
        self.send(31 + k, self.block(tid), p.partner)

    def step_partner(self, k):
        p = self.place
        for j, shift in enumerate((0, 3, 1, 2)):
            tid = p.tid(p.ysrc(k), p.xat(shift), 1 - p.c)
            self.wait(19 + 4 * j + k, self.block(tid), p.partner)


class Place:
    def __init__(self):
        self.dp = lax.axis_index("dp")
        self.t = lax.axis_index("tensor")
        self.c = lax.rem(self.t, 2)
        self.x = lax.rem(lax.div(self.t, 2), 4)
        self.y = lax.div(self.t, 8)
        self.left = self.tid(self.y, self.xat(3), self.c)
        self.right = self.tid(self.y, self.xat(1), self.c)
        self.partner = self.tid(self.y, self.x, 1 - self.c)
        self.pair = lax.div(self.x, 2)
        self.kind = lax.rem(self.x, 2)
        self.mirror = self.tid(self.y, 3 - self.x, self.c)
        self.mate = self.tid(self.y, self.x + 1 - 2 * self.kind, self.c)

    def tid(self, y, x, c):
        return (y * 4 + x) * 2 + c

    def xat(self, shift):
        return lax.rem(self.x + shift, 4)

    def ydst(self, k):
        return lax.rem(self.y + k, 4)

    def ysrc(self, k):
        return lax.rem(self.y + 4 - k, 4)


def kernel(
    slots_in, lengths_in, owners_in, gain_in, wq_in, qbias_in, wkv_in, kvbias_in, up_in, cos_in, sin_in,
    att_out, grad_out,
    slots, lengths, owners, gain, wq, qbias, wkv, kvbias, up, cos16, sin16, att, grad,
    a_send, a_recv, full, acc, ssq,
    d0_send, d0_recv, d_own, d1_send, d1_recv, d2_send, d2_recv, d3_send, d3_recv, kvraw,
    cos_s, sin_s, q_grad, kv_f32, e1_send, e1_recv, e_sum, e2_send, e2_recv, ebuf, rs_rows, kvfull,
    f0_send, f0_recv, far_send, far_l, far_r, r_send, l_send, from_l, from_r, s_own, s_r, s_l, y_send, y_recv,
    local_sem, a_ss, a_rs, b_ss, b_rs, d_ss, d_rs, e_ss, e_rs, g_ss, g_rs, f_ss, f_rs,
):
    p = Place()
    dp, t, c = p.dp, p.t, p.c

    barrier = pltpu.get_barrier_semaphore()

    def greet(k, carry):
        pl.semaphore_signal(barrier, inc=1, device_id=(lax.rem(dp + k, N_DP), t), device_id_type=MESH)
        return carry

    lax.fori_loop(1, N_DP, greet, 0)
    for peer in (p.partner, p.left, p.right) + tuple(p.tid(p.ydst(k), p.x, c) for k in (1, 2, 3)):
        pl.semaphore_signal(barrier, inc=1, device_id=(dp, peer), device_id_type=MESH)

    pairs = (
        (owners_in, owners), (slots_in, slots), (lengths_in, lengths), (gain_in, gain), (wkv_in, wkv),
        (kvbias_in, kvbias), (qbias_in, qbias), (cos_in, cos16), (sin_in, sin16), (up_in, up), (wq_in, wq),
    )
    loads = [pltpu.make_async_copy(a, b, local_sem.at[i]) for i, (a, b) in enumerate(pairs)]
    for one in loads:
        one.start()

    total = N_DP * WINDOW
    row_of = (lax.div(iota((total, N_DP), 0), WINDOW) == iota((total, N_DP), 1)).astype(F32).astype(BF16)
    col_of = (lax.div(iota((N_DP, total), 1), WINDOW) == iota((N_DP, total), 0)).astype(F32).astype(BF16)
    same_row = lax.rem(iota((total, total), 0), WINDOW) == lax.rem(iota((total, total), 1), WINDOW)
    loads[0].wait()
    owner_f = owners[...].astype(F32)
    mine = (mm(row_of, owner_f.astype(BF16)) == dp.astype(F32)).astype(F32).astype(BF16)
    pick = jnp.where(same_row, mm(mine, col_of), 0.0).astype(BF16)
    loads[1].wait()
    outgoing = mm(pick, slots[...].reshape(total, PART)).astype(BF16).reshape(N_DP, WINDOW, PART)
    a_send[...] = outgoing
    a_recv[dp] = a_send[dp]
    pl.semaphore_wait(barrier, N_DP - 1 + 6)

    def rollout(src, dst, k, peer):
        return pltpu.make_async_remote_copy(
            src_ref=src, dst_ref=dst, send_sem=a_ss.at[k], recv_sem=a_rs.at[k], device_id=(peer, t), device_id_type=MESH
        )

    def send_rollout(k, carry):
        peer = lax.rem(dp + k, N_DP)
        rollout(a_send.at[peer], a_recv.at[dp], k, peer).start()
        return carry

    def wait_rollout(k, carry):
        peer = lax.rem(dp + N_DP - k, N_DP)
        rollout(a_recv.at[peer], a_recv.at[peer], k, peer).wait_recv()
        return carry

    def drain_rollout(k, carry):
        peer = lax.rem(dp + k, N_DP)
        rollout(a_send.at[peer], a_recv.at[dp], k, peer).wait_send()
        return carry

    lax.fori_loop(1, N_DP, send_rollout, 0)

    for one in loads[2:]:
        one.wait()
    length_row = jnp.broadcast_to(lengths[pl.ds(dp, 1), :].astype(F32), (ROWS, N_DP))
    owner_row = jnp.broadcast_to(owners[pl.ds(dp, 1), :].astype(F32), (ROWS, N_DP))
    before = (iota((N_DP, N_DP), 0) < iota((N_DP, N_DP), 1)).astype(F32).astype(BF16)
    starts = mm(length_row.astype(BF16), before)
    place = iota((ROWS, N_DP), 0).astype(F32)
    inside = (place >= starts) & (place < starts + length_row)
    start = jnp.sum(jnp.where(inside, starts, 0.0), axis=1, keepdims=True)
    source = jnp.sum(jnp.where(inside, owner_row, 0.0), axis=1, keepdims=True)
    offset = iota((ROWS, 1), 0).astype(F32) - start
    wanted = (source * WINDOW + offset).astype(jnp.int32)
    select = (iota((ROWS, total), 1) == wanted).astype(F32).astype(BF16)
    turn = (iota((ROWS, WINDOW), 1) == offset.astype(jnp.int32)).astype(F32)
    sign = jnp.where(iota((ROWS, HEAD_DIM), 1) < HALF_DIM, -1.0, 1.0)
    cos_s[...] = exact_mm(turn, cos16[...])
    sin_s[...] = exact_mm(turn, sin16[...])
    key_place = iota((ROWS, ROWS), 1)
    allowed = (key_place >= start.astype(jnp.int32)) & (key_place <= iota((ROWS, ROWS), 0))
    acc[...] = jnp.zeros_like(acc)
    ssq[...] = jnp.zeros_like(ssq)
    own_gain = jnp.concatenate([gain[pl.ds(2 * t, 1), :], gain[pl.ds(2 * t + 1, 1), :]], axis=1)

    lax.fori_loop(1, N_DP, wait_rollout, 0)
    hidden = mm(select, a_recv[...].reshape(total, PART))
    full[t] = hidden.astype(BF16)

    links = Links(dp)
    tree = Tree(links, p, full, HALF, b_ss, b_rs)
    tree.start()

    scaled_local = (hidden * own_gain).astype(BF16)

    def project(i, carry):
        for own, col in ((True, c * 1024 + i * 256), (False, (1 - c) * 1024 + i * 256)):
            value = mm(scaled_local, wkv[:, pl.ds(pl.multiple_of(col, 256), 256)])
            if own:
                d_own[2 * i] = value[:, :128]
                d_own[2 * i + 1] = value[:, 128:]
            else:
                d0_send[2 * i] = value[:, :128].astype(BF16)
                d0_send[2 * i + 1] = value[:, 128:].astype(BF16)
        return carry

    lax.fori_loop(0, 4, project, 0)
    links.send(d0_send, d0_recv, d_ss.at[0], d_rs.at[0], p.partner)

    def consume(core, k):
        def body(j, carry):
            tid = p.tid(p.ysrc(k), lax.rem(p.x + j, 4), core)
            block = full[tid].astype(F32)
            low, high = block[:, :128], block[:, 128:]
            ssq[...] += low * low + high * high
            scaled = jnp.concatenate(
                [low * gain[pl.ds(2 * tid, 1), :], high * gain[pl.ds(2 * tid + 1, 1), :]], axis=1
            ).astype(BF16)
            acc[...] += mm(scaled, wq[pl.ds(pl.multiple_of(tid * PART, PART), PART), :])
            return carry

        lax.fori_loop(0, 4, body, 0)

    tree.step_y(1)
    tree.step_x(0)
    links.wait(d0_recv, d_ss.at[0], d_rs.at[0], p.partner)
    for i in range(4):
        g = 2 * i + 1 - p.pair
        d1_send[i] = (d_own[g] + d0_recv[g].astype(F32)).astype(BF16)
    links.send(d1_send, d1_recv, d_ss.at[1], d_rs.at[1], p.mirror)
    tree.step_y(2)
    tree.step_x(1)
    tree.step_far(0)
    consume(c, 0)
    links.wait(d1_recv, d_ss.at[1], d_rs.at[1], p.mirror)

    def pair_sum(i):
        g = 2 * i + p.pair
        return d_own[g] + d0_recv[g].astype(F32) + d1_recv[i].astype(F32)

    for k in (1, 2, 3):
        d2_send[k] = pair_sum(p.ydst(k)).astype(BF16)
        links.send(d2_send.at[k], d2_recv.at[k], d_ss.at[1 + k], d_rs.at[1 + k], p.tid(p.ydst(k), p.x, c))
    tree.step_y(3)
    tree.step_x(2)
    tree.step_far(1)
    consume(c, 1)
    column = pair_sum(p.y)
    for k in (1, 2, 3):
        links.wait(d2_recv.at[k], d_ss.at[1 + k], d_rs.at[1 + k], p.tid(p.ysrc(k), p.x, c))
        column = column + d2_recv[k].astype(F32)
    d3_send[...] = column.astype(BF16)
    links.send(d3_send, d3_recv, d_ss.at[5], d_rs.at[5], p.mate)
    tree.step_x(3)
    tree.step_far(2)
    tree.step_partner(0)
    consume(1 - c, 0)
    consume(c, 2)
    links.wait(d3_recv, d_ss.at[5], d_rs.at[5], p.mate)
    kvraw[c] = column + d3_recv[...].astype(F32)
    links.send(kvraw.at[c], kvraw.at[c], d_ss.at[6], d_rs.at[6], p.partner)
    tree.step_partner(1)
    consume(1 - c, 1)
    tree.step_far(3)
    consume(c, 3)
    tree.step_partner(2)
    consume(1 - c, 2)
    tree.step_partner(3)
    consume(1 - c, 3)
    links.wait(kvraw.at[1 - c], d_ss.at[6], d_rs.at[6], p.partner)

    cosine, sine = cos_s[...], sin_s[...]
    inverse = lax.rsqrt(jnp.sum(ssq[...], axis=1, keepdims=True) * (1.0 / D) + EPSILON)

    def rotate(u):
        return u * cosine + pltpu.roll(u, HALF_DIM, 1) * (sign * sine)

    def unrotate(z, cosine, sine, sign):
        return z * cosine - pltpu.roll(z * sine, HALF_DIM, 1) * sign

    group = p.y * 2 + p.pair
    key_raw, value_raw = kvraw[0], kvraw[1]
    key = rotate(inverse * key_raw + kvbias[pl.ds(group, 1), :]).astype(BF16)
    value = (inverse * value_raw + kvbias[pl.ds(KV_HEADS + group, 1), :]).astype(BF16)
    query = jnp.concatenate(
        [rotate(inverse * acc[:, h * 128 : h * 128 + 128] + qbias[h : h + 1, :]).astype(BF16) for h in (0, 1)], axis=0
    )
    upstream = jnp.concatenate([up[:, :128], up[:, 128:]], axis=0)
    both = jnp.concatenate([allowed.astype(F32), allowed.astype(F32)], axis=0) > 0.5
    scores = jnp.where(both, mm_nt(query, key) * SCALE, -1e30)
    highest = jnp.max(scores, axis=1, keepdims=True)
    exponent = jnp.where(both, jnp.exp(scores - highest), 0.0)
    weights = exponent / jnp.sum(exponent, axis=1, keepdims=True)
    low = weights.astype(BF16)
    attended = mm(low, value).astype(BF16)
    att[:, :128] = attended[:ROWS]
    att[:, 128:] = attended[ROWS:]
    att_copy = pltpu.make_async_copy(att, att_out, local_sem.at[11])
    att_copy.start()
    weight_grad = mm_nt(upstream, value)
    inner = jnp.sum(weights * weight_grad, axis=1, keepdims=True)
    score_grad = (weights * (weight_grad - inner) * SCALE).astype(BF16)
    kv_f32[0] = mm_tn(score_grad, query)
    kv_f32[1] = mm_tn(low, upstream)
    e1_send[...] = kv_f32[...].astype(BF16)
    other = pl.multiple_of((1 - c) * HALF, HALF)
    links.send(e1_send.at[:, pl.ds(other, HALF), :], e1_recv, g_ss.at[0], g_rs.at[0], p.partner)
    query_grad = mm(score_grad, key)
    for h in (0, 1):
        piece = unrotate(query_grad[h * ROWS : h * ROWS + ROWS], cosine, sine, sign).astype(BF16)
        q_grad[:, h * 128 : h * 128 + 128] = piece
        product = piece.astype(F32) * acc[:, h * 128 : h * 128 + 128]
        if h == 0:
            rs_rows[pl.ds(0, ROWS), :] = product
        else:
            rs_rows[pl.ds(0, ROWS), :] += product
    rs_rows[pl.ds(ROWS, 64), :] = jnp.zeros((64, 128), F32)

    def partial(k, shift, core):
        tid = p.tid(p.ydst(k), lax.rem(p.x + shift, 4), core)
        return mm_nt(q_grad[...], wq[pl.ds(pl.multiple_of(tid * PART, PART), PART), :])

    def f_cores(k):
        def body(j, carry):
            f0_send[k, j] = partial(k, j, 1 - c).astype(BF16)
            return carry

        lax.fori_loop(0, 4, body, 0)
        links.send(f0_send.at[k], f0_recv.at[k], f_ss.at[k], f_rs.at[k], p.partner)

    top, bottom = pl.ds(0, HALF), pl.ds(HALF, HALF)

    def f_first(k):
        links.wait(f0_recv.at[k], f_ss.at[k], f_rs.at[k], p.partner)
        far_send[k] = (partial(k, 2, c) + f0_recv[k, 2].astype(F32)).astype(BF16)
        links.send(far_send.at[k, top], far_l.at[k], f_ss.at[4 + k], f_rs.at[4 + k], p.right)
        links.send(far_send.at[k, bottom], far_r.at[k], f_ss.at[8 + k], f_rs.at[8 + k], p.left)
        value = partial(k, 1, c) + f0_recv[k, 1].astype(F32)
        r_send[k, bottom] = value[HALF:].astype(BF16)
        links.send(r_send.at[k, bottom], from_l.at[k, bottom], f_ss.at[12 + k], f_rs.at[12 + k], p.right)
        s_r[k] = value[:HALF]
        value = partial(k, 3, c) + f0_recv[k, 3].astype(F32)
        l_send[k, top] = value[:HALF].astype(BF16)
        links.send(l_send.at[k, top], from_r.at[k, top], f_ss.at[16 + k], f_rs.at[16 + k], p.left)
        s_l[k] = value[HALF:]
        s_own[k] = partial(k, 0, c) + f0_recv[k, 0].astype(F32)

    def f_second(k):
        links.wait(far_l.at[k], f_ss.at[4 + k], f_rs.at[4 + k], p.left)
        r_send[k, top] = (s_r[k] + far_l[k].astype(F32)).astype(BF16)
        links.send(r_send.at[k, top], from_l.at[k, top], f_ss.at[20 + k], f_rs.at[20 + k], p.right)
        links.wait(far_r.at[k], f_ss.at[8 + k], f_rs.at[8 + k], p.right)
        l_send[k, bottom] = (s_l[k] + far_r[k].astype(F32)).astype(BF16)
        links.send(l_send.at[k, bottom], from_r.at[k, bottom], f_ss.at[24 + k], f_rs.at[24 + k], p.left)

    def f_third(k):
        links.wait(from_l.at[k, bottom], f_ss.at[12 + k], f_rs.at[12 + k], p.left)
        links.wait(from_r.at[k, top], f_ss.at[16 + k], f_rs.at[16 + k], p.right)
        links.wait(from_l.at[k, top], f_ss.at[20 + k], f_rs.at[20 + k], p.left)
        links.wait(from_r.at[k, bottom], f_ss.at[24 + k], f_rs.at[24 + k], p.right)
        value = s_own[k] + from_l[k].astype(F32) + from_r[k].astype(F32)
        if k == 0:
            s_own[k] = value
        else:
            y_send[k] = value.astype(BF16)
            links.send(
                y_send.at[k], y_recv.at[k], f_ss.at[28 + k], f_rs.at[28 + k], p.tid(p.ydst(k), p.x, c)
            )

    grads = Tree(links, p, ebuf, 64, e_ss, e_rs)
    f_cores(1)
    f_cores(2)
    links.wait(e1_recv, g_ss.at[0], g_rs.at[0], p.partner)
    mine_rows = pl.ds(pl.multiple_of(c * HALF, HALF), HALF)
    e_sum[...] = kv_f32[:, mine_rows, :] + e1_recv[...].astype(F32)
    e2_send[...] = e_sum[...].astype(BF16)
    links.send(e2_send.at[1 - p.kind], e2_recv, g_ss.at[1], g_rs.at[1], p.mate)
    f_first(1)
    f_cores(3)
    f_first(2)
    links.wait(e2_recv, g_ss.at[1], g_rs.at[1], p.mate)
    value_side = p.kind.astype(F32)
    half_sign = sign[:HALF]
    finished = unrotate(
        e_sum[p.kind] + e2_recv[...].astype(F32),
        cos_s[mine_rows, :] * (1.0 - value_side) + value_side,
        sin_s[mine_rows, :] * (1.0 - value_side),
        half_sign,
    ).astype(BF16)
    rs_rows[mine_rows, :] += finished.astype(F32) * kvraw[p.kind, mine_rows, :]
    ones = jnp.ones((8, 128), F32)
    stat = jnp.concatenate([exact_nt(ones, rs_rows[0:128, :]), exact_nt(ones, rs_rows[128:256, :])], axis=0)
    coarse = stat.astype(BF16).astype(F32)
    ebuf[t, pl.ds(0, HALF)] = finished
    ebuf[t, pl.ds(HALF, 16)] = jnp.where(lax.rem(iota((16, 128), 0), 2) == 0, coarse, stat - coarse).astype(BF16)
    grads.start()
    f_cores(0)
    f_second(1)
    f_first(3)
    f_second(2)
    f_third(1)
    grads.step_y(1)
    f_first(0)
    f_second(3)
    f_third(2)
    grads.step_y(2)
    grads.step_x(0)
    f_second(0)
    grads.step_y(3)
    grads.step_x(1)
    grads.step_far(0)
    f_third(3)
    grads.step_x(2)
    grads.step_far(1)
    grads.step_x(3)
    grads.step_far(2)
    grads.step_far(3)
    f_third(0)
    for k in range(4):
        grads.step_partner(k)

    def place_grad(tid, carry):
        core = lax.rem(tid, 2)
        xs = lax.rem(lax.div(tid, 2), 4)
        ys = lax.div(tid, 8)
        col = lax.rem(xs, 2) * 1024 + (ys * 2 + lax.div(xs, 2)) * 128
        kvfull[pl.ds(pl.multiple_of(core * HALF, HALF), HALF), pl.ds(pl.multiple_of(col, 128), 128)] = ebuf[
            tid, pl.ds(0, HALF)
        ]
        return carry + ebuf[tid, pl.ds(HALF, 16)].astype(F32)

    stats = lax.fori_loop(0, LANES, place_grad, jnp.zeros((16, 128), F32))
    key_value_part = mm_nt(kvfull[...], wkv[...])
    eye = iota((128, 128), 0) == iota((128, 128), 1)

    def upright(row):
        return jnp.sum(jnp.where(eye, jnp.broadcast_to(row, (128, 128)), 0.0), axis=1, keepdims=True)

    row_stat = jnp.concatenate(
        [upright(stats[0:1] + stats[1:2]), upright(stats[8:9] + stats[9:10])[: ROWS - 128]], axis=0
    ) * (1.0 / D)
    normed_grad = s_own[0] + key_value_part
    for k in (1, 2, 3):
        links.wait(y_recv.at[k], f_ss.at[28 + k], f_rs.at[28 + k], p.tid(p.ysrc(k), p.x, c))
        normed_grad = normed_grad + y_recv[k].astype(F32)
    own_gain = jnp.concatenate([gain[pl.ds(2 * t, 1), :], gain[pl.ds(2 * t + 1, 1), :]], axis=1)
    grad[...] = (
        inverse * (own_gain * normed_grad)
        - full[t].astype(F32) * (inverse * inverse * inverse * row_stat)
    ).astype(BF16)
    grad_copy = pltpu.make_async_copy(grad, grad_out, local_sem.at[12])
    grad_copy.start()
    lax.fori_loop(1, N_DP, drain_rollout, 0)
    links.drain()
    att_copy.wait()
    grad_copy.wait()


def on_device(
    hidden_slots, lengths, owners, norm_gain, w_query, query_bias, w_keyvalue, keyvalue_bias, grad_attention
):
    frequency = ROPE_BASE ** (-2.0 * np.arange(HALF_DIM, dtype=np.float32) / HEAD_DIM)
    angles = np.arange(WINDOW, dtype=np.float32)[:, None] * frequency[None, :].astype(np.float32)
    angles = np.concatenate([angles, angles], axis=1)
    cosine = jnp.asarray(np.cos(angles), F32)
    sine = jnp.asarray(np.sin(angles), F32)
    operands = (
        hidden_slots, lengths, owners, norm_gain.reshape(64, 128), w_query, query_bias.reshape(2, 128),
        w_keyvalue, keyvalue_bias.reshape(16, 128), grad_attention, cosine, sine,
    )

    def v(*shape, dtype=BF16):
        return pltpu.VMEM(shape, dtype)

    def dma(n):
        return pltpu.SemaphoreType.DMA((n,))

    scratch = [pltpu.VMEM(one.shape, one.dtype) for one in operands]
    scratch += [v(ROWS, PART), v(ROWS, PART)]
    scratch += [
        v(N_DP, WINDOW, PART), v(N_DP, WINDOW, PART), v(LANES, ROWS, PART), v(ROWS, PART, dtype=F32),
        v(ROWS, 128, dtype=F32),
    ]
    scratch += [
        v(8, ROWS, 128), v(8, ROWS, 128), v(8, ROWS, 128, dtype=F32), v(4, ROWS, 128), v(4, ROWS, 128),
        v(4, ROWS, 128), v(4, ROWS, 128), v(ROWS, 128), v(ROWS, 128), v(2, ROWS, 128, dtype=F32),
    ]
    scratch += [
        v(ROWS, 128, dtype=F32), v(ROWS, 128, dtype=F32), v(ROWS, PART), v(2, ROWS, 128, dtype=F32),
        v(2, ROWS, 128), v(2, HALF, 128), v(2, HALF, 128, dtype=F32), v(2, HALF, 128), v(HALF, 128),
        v(LANES, GRAD_ROWS, 128), v(256, 128, dtype=F32), v(ROWS, 2048),
    ]
    scratch += [
        v(4, 4, ROWS, PART), v(4, 4, ROWS, PART), v(4, ROWS, PART), v(4, HALF, PART), v(4, HALF, PART),
        v(4, ROWS, PART), v(4, ROWS, PART), v(4, ROWS, PART), v(4, ROWS, PART), v(4, ROWS, PART, dtype=F32),
        v(4, HALF, PART, dtype=F32), v(4, HALF, PART, dtype=F32), v(4, ROWS, PART), v(4, ROWS, PART),
    ]
    scratch += [
        dma(13), dma(N_DP), dma(N_DP), dma(TREE_SLOTS), dma(TREE_SLOTS), dma(7), dma(7),
        dma(TREE_SLOTS), dma(TREE_SLOTS), dma(2), dma(2), dma(32), dma(32),
    ]
    shape = jax.ShapeDtypeStruct((ROWS, PART), BF16)
    return pl.pallas_call(
        kernel,
        out_shape=(shape, shape),
        in_specs=[pl.BlockSpec(memory_space=pl.ANY)] * len(operands),
        out_specs=[pl.BlockSpec(memory_space=pl.ANY)] * 2,
        scratch_shapes=scratch,
        compiler_params=pltpu.CompilerParams(
            collective_id=0, has_side_effects=True, vmem_limit_bytes=60 * 1024 * 1024
        ),
        name="step",
    )(*operands)


def solution(mesh):
    in_specs = (
        P("dp", None, "tensor"),
        P(),
        P(),
        P(),
        P(None, "tensor"),
        P("tensor"),
        P("tensor", None),
        P(),
        P("dp", "tensor"),
    )
    out_specs = (P("dp", "tensor"), P("dp", "tensor"))
    return jax.shard_map(on_device, mesh=mesh, in_specs=in_specs, out_specs=out_specs, check_vma=False)
```

time: 485 us -> 92.2 us (0.19)
  waiting for transfers between devices: 278 us -> 0 us
  Pallas kernels: 0 us -> 88.3 us
  blocking collectives: 78.2 us -> 0 us
  starting transfers between devices: 64.5 us -> 0 us
  matrix products: 18.9 us -> 0 us
  local copies, waits for them, and re-layouts: 20.7 us -> 3.08 us
  between operations: 15 us -> 0.64 us
  other arithmetic: 9.29 us -> 0 us
    all_gather x2 -> x0, waiting for transfers between devices: 127 us -> none  [the longest x1 66.3 us: on_device(): full_rows = lax.all_gather(local_rows, 'tensor', axis=1, tiled=True)]
    all_to_all x4 -> x0, waiting for transfers between devices: 101 us -> none  [the longest x1 54.4 us: sum_at_owner(): lax.all_to_all(tiles, axis, split_axis=0, concat_axis=0, tiled=True)]
    pallas_call x0 -> x1, Pallas kernels: none -> 88.3 us  [on_device(): pl.pallas_call(kernel, out_shape=(shape, shape), in_specs=[pl.BlockSpec(m...]
    unnamed x1 -> x0, blocking collectives: 78.2 us -> none
    reduce_scatter x1 -> x0, waiting for transfers between devices: 49.2 us -> none  [on_device(): lax.psum_scatter(query_part.astype(jnp.bfloat16), 'tensor', scatter_dimen...]
    all_to_all x4 -> x0, starting transfers between devices: 40 us -> none  [the longest x1 21.2 us: on_device(): lax.all_to_all(outgoing, 'dp', split_axis=0, concat_axis=0, tiled=True)]
    unnamed x8 -> x0, starting transfers between devices: 24.4 us -> none
    dot_general x10 -> x0, matrix products: 17.7 us -> none  [the longest x2 6.9 us: contract_last(): lax.dot_general(operand, weights, (((1,), (1,)), ((), ())), preferred_ele...]
  transfers between devices with their start and end apart: 15 -> 0, of which waited for: 7 -> 0; matrix products, arithmetic and copies ran while one was open for 5% -> 0% of each run, Pallas kernels for 0% -> 0%
where the time goes in v1:
time: 92.2 us; the launch traced here: 92 us
  Pallas kernels  88.3 us (96%)
  local copies, waits for them, and re-layouts  3.08 us (3%)
    pallas_call x1, Pallas kernels, on_device(): pl.pallas_call(kernel, out_shape=(shape, shape), in_specs=[pl.BlockSpec(m...  88.3 us
    unnamed x2, local copies, waits for them, and re-layouts  3.08 us

profile of v1, /device:TPU:1, one launch (start us, length us, event | category | flops | bytes accessed | tf_op | source)
XLA Modules:
  0.0 92.0 jit_solution(16798770622660138359)
XLA Ops:
  0.6 88.3 %step.1 = (bf16[192,256]{1,0:T(8,128)(2,1)}, bf16[192,256]{1,0:T(8,128)(2,1)}) custom-call(bf16[24,16,256]{2,1,0:T(8,128)(2,1)} %slots_in.1, s32[24,24]{1,0:T(8,128)} %lengths_in.1, s32[24,24]{1,0:T(8,128)} %owners_in.1, f32[64,128]{1,0:T(8,128)} %bitcast.3, bf16[8192,256]{1,0:T(8,128)(2,1)} %wq_in.1, f32[2,128]{1,0:T(2,128)} %bitcast.5, ...), custom_call_target="tpu_custom_call" | custom-call | tf_op jit(solution)/shard_map/step/pallas_call | solution.py:590
  89.0 1.5 %copy.15 = bf16[192,256]{1,0:T(8,128)(2,1)} copy(bf16[192,256]{1,0:T(8,128)(2,1)} %get-tuple-element.4) | data formatting | bytes 196608
  90.5 1.5 %copy.16 = bf16[192,256]{1,0:T(8,128)(2,1)} copy(bf16[192,256]{1,0:T(8,128)(2,1)} %get-tuple-element.5) | data formatting | bytes 196608

commit v2 on v1

--- a/solution.py
+++ b/solution.py
@@ -23,8 +23,8 @@
 MESH = pl.DeviceIdType.MESH
 F32 = jnp.float32
 BF16 = jnp.bfloat16
-TREE_SLOTS = 35
-GRAD_ROWS = HALF + 16
+TREE_SLOTS = 39
+GRAD_ROWS = ROWS + 16
 ORDER = (1, 2, 3, 0)
 
 
@@ -85,11 +85,11 @@
 
 
 class Tree:
-    def __init__(self, links, place, buffer, split, send_sems, recv_sems):
+    def __init__(self, links, place, buffer, cuts, send_sems, recv_sems):
         self.links = links
         self.place = place
         self.buffer = buffer
-        self.split = split
+        self.cuts = cuts
         self.ss = send_sems
         self.rs = recv_sems
 
@@ -97,10 +97,9 @@
         return self.buffer.at[tid]
 
     def part(self, tid, which):
-        size = self.buffer.shape[1]
-        if which == 0:
-            return self.buffer.at[tid, pl.ds(0, self.split)]
-        return self.buffer.at[tid, pl.ds(self.split, size - self.split)]
+        low, high = self.cuts
+        begin, size = ((0, low), (low, high - low), (high, self.buffer.shape[1] - high))[which]
+        return self.buffer.at[tid, pl.ds(begin, size)]
 
     def send(self, slot, ref, peer):
         self.links.send(ref, ref, self.ss.at[slot], self.rs.at[slot], peer)
@@ -129,27 +128,36 @@
 
     def step_x(self, k):
         p = self.place
-        tid = p.tid(p.ysrc(k), p.xat(3), p.c)
-        self.wait(3 + k, self.block(tid), p.left)
-        self.send(11 + k, self.part(tid, 0), p.right)
-        self.send(23 + k, self.block(tid), p.partner)
-        tid = p.tid(p.ysrc(k), p.xat(1), p.c)
-        self.wait(7 + k, self.block(tid), p.right)
-        self.send(15 + k, self.part(tid, 1), p.left)
-        self.send(27 + k, self.block(tid), p.partner)
+        left = p.tid(p.ysrc(k), p.xat(3), p.c)
+        right = p.tid(p.ysrc(k), p.xat(1), p.c)
+        self.wait(3 + k, self.block(left), p.left)
+        self.send(11 + k, self.part(left, 0), p.right)
+        self.wait(7 + k, self.block(right), p.right)
+        self.send(15 + k, self.part(right, 2), p.left)
+        self.send(35 + k, self.part(p.tid(p.ysrc(k), 3 - p.x, p.c), 1), p.mate)
+        self.send(23 + k, self.block(left), p.partner)
+        self.send(27 + k, self.block(right), p.partner)
 
     def step_far(self, k):
         p = self.place
         tid = p.tid(p.ysrc(k), p.xat(2), p.c)
         self.wait(11 + k, self.part(tid, 0), p.left)
-        self.wait(15 + k, self.part(tid, 1), p.right)
+        self.wait(15 + k, self.part(tid, 2), p.right)
+        self.wait(35 + k, self.part(tid, 1), p.mate)
         self.send(31 + k, self.block(tid), p.partner)
 
-    def step_partner(self, k):
+    def partner_wait(self, k, which):
         p = self.place
         for j, shift in enumerate((0, 3, 1, 2)):
-            tid = p.tid(p.ysrc(k), p.xat(shift), 1 - p.c)
-            self.wait(19 + 4 * j + k, self.block(tid), p.partner)
+            if j in which:
+                tid = p.tid(p.ysrc(k), p.xat(shift), 1 - p.c)
+                self.wait(19 + 4 * j + k, self.block(tid), p.partner)
+
+    def partner_near(self, k):
+        self.partner_wait(k, (0, 1, 2))
+
+    def partner_far(self, k):
+        self.partner_wait(k, (3,))
 
 
 class Place:
@@ -165,7 +173,12 @@
         self.pair = lax.div(self.x, 2)
         self.kind = lax.rem(self.x, 2)
         self.mirror = self.tid(self.y, 3 - self.x, self.c)
+        self.mirror_other = self.tid(self.y, 3 - self.x, 1 - self.c)
+        self.row_index = self.x * 2 + self.c
         self.mate = self.tid(self.y, self.x + 1 - 2 * self.kind, self.c)
+
+    def in_row(self, j):
+        return self.y * 8 + lax.rem(self.row_index + j, 8)
 
     def tid(self, y, x, c):
         return (y * 4 + x) * 2 + c
@@ -174,21 +187,27 @@
         return lax.rem(self.x + shift, 4)
 
     def ydst(self, k):
-        return lax.rem(self.y + k, 4)
+        if k == 3:
+            return 3 - self.y
+        if k == 2:
+            return self.y + 2 - 4 * lax.div(self.y, 2)
+        if k == 1:
+            return self.y + 1 - 2 * lax.rem(self.y, 2)
+        return self.y
 
     def ysrc(self, k):
-        return lax.rem(self.y + 4 - k, 4)
+        return self.ydst(k)
 
 
 def kernel(
     slots_in, lengths_in, owners_in, gain_in, wq_in, qbias_in, wkv_in, kvbias_in, up_in, cos_in, sin_in,
     att_out, grad_out,
-    slots, lengths, owners, gain, wq, qbias, wkv, kvbias, up, cos16, sin16, att, grad,
+    slots, lengths, owners, gain, wq, qbias, kvbias, up, cos16, sin16, att, grad,
     a_send, a_recv, full, acc, ssq,
-    d0_send, d0_recv, d_own, d1_send, d1_recv, d2_send, d2_recv, d3_send, d3_recv, kvraw,
-    cos_s, sin_s, q_grad, kv_f32, e1_send, e1_recv, e_sum, e2_send, e2_recv, ebuf, rs_rows, kvfull,
+    w_own, w_far, d_own, d2_send, d2_recv, d3_send, d3_recv, kvraw,
+    cos_s, sin_s, q_grad, kv_f32, e1_send, e1_recv, e2_send, e2_recv, ebuf, rs_rows, rs_all, kv_part, products_s,
     f0_send, f0_recv, far_send, far_l, far_r, r_send, l_send, from_l, from_r, s_own, s_r, s_l, y_send, y_recv,
-    local_sem, a_ss, a_rs, b_ss, b_rs, d_ss, d_rs, e_ss, e_rs, g_ss, g_rs, f_ss, f_rs,
+    local_sem, a_ss, a_rs, b_ss, b_rs, d_ss, d_rs, e_ss, e_rs, r_ss, r_rs, c_ss, c_rs, f_ss, f_rs,
 ):
     p = Place()
     dp, t, c = p.dp, p.t, p.c
@@ -200,14 +219,24 @@
         return carry
 
     lax.fori_loop(1, N_DP, greet, 0)
-    for peer in (p.partner, p.left, p.right) + tuple(p.tid(p.ydst(k), p.x, c) for k in (1, 2, 3)):
+    for peer in tuple(p.in_row(j) for j in range(1, 8)) + tuple(p.tid(p.ydst(k), p.x, c) for k in (1, 2, 3)):
         pl.semaphore_signal(barrier, inc=1, device_id=(dp, peer), device_id_type=MESH)
 
     pairs = (
-        (owners_in, owners), (slots_in, slots), (lengths_in, lengths), (gain_in, gain), (wkv_in, wkv),
+        (owners_in, owners), (slots_in, slots), (lengths_in, lengths), (gain_in, gain),
         (kvbias_in, kvbias), (qbias_in, qbias), (cos_in, cos16), (sin_in, sin16), (up_in, up), (wq_in, wq),
     )
     loads = [pltpu.make_async_copy(a, b, local_sem.at[i]) for i, (a, b) in enumerate(pairs)]
+    for kind in (0, 1):
+        for pair in (0, 1):
+            for i in range(4):
+                loads.append(
+                    pltpu.make_async_copy(
+                        wkv_in.at[:, pl.ds(kind * 1024 + (2 * i + pair) * 128, 128)],
+                        w_own.at[kind, pair, :, pl.ds(i * 128, 128)],
+                        local_sem.at[12 + kind * 8 + pair * 4 + i],
+                    )
+                )
     for one in loads:
         one.start()
 
@@ -223,7 +252,7 @@
     outgoing = mm(pick, slots[...].reshape(total, PART)).astype(BF16).reshape(N_DP, WINDOW, PART)
     a_send[...] = outgoing
     a_recv[dp] = a_send[dp]
-    pl.semaphore_wait(barrier, N_DP - 1 + 6)
+    pl.semaphore_wait(barrier, N_DP - 1 + 10)
 
     def rollout(src, dst, k, peer):
         return pltpu.make_async_remote_copy(
@@ -249,6 +278,11 @@
 
     for one in loads[2:]:
         one.wait()
+    links = Links(dp)
+    links.send(w_own.at[1 - c, p.pair], w_far.at[0], d_ss.at[0], d_rs.at[0], p.partner)
+    links.send(w_own.at[c, 1 - p.pair], w_far.at[1], d_ss.at[1], d_rs.at[1], p.mirror)
+    links.send(w_own.at[1 - c, 1 - p.pair], w_far.at[2], d_ss.at[7], d_rs.at[7], p.mirror_other)
+
     length_row = jnp.broadcast_to(lengths[pl.ds(dp, 1), :].astype(F32), (ROWS, N_DP))
     owner_row = jnp.broadcast_to(owners[pl.ds(dp, 1), :].astype(F32), (ROWS, N_DP))
     before = (iota((N_DP, N_DP), 0) < iota((N_DP, N_DP), 1)).astype(F32).astype(BF16)
@@ -268,92 +302,86 @@
     allowed = (key_place >= start.astype(jnp.int32)) & (key_place <= iota((ROWS, ROWS), 0))
     acc[...] = jnp.zeros_like(acc)
     ssq[...] = jnp.zeros_like(ssq)
-    own_gain = jnp.concatenate([gain[pl.ds(2 * t, 1), :], gain[pl.ds(2 * t + 1, 1), :]], axis=1)
+    kv_part[...] = jnp.zeros_like(kv_part)
 
     lax.fori_loop(1, N_DP, wait_rollout, 0)
     hidden = mm(select, a_recv[...].reshape(total, PART))
     full[t] = hidden.astype(BF16)
 
-    links = Links(dp)
-    tree = Tree(links, p, full, HALF, b_ss, b_rs)
+    tree = Tree(links, p, full, (80, 112), b_ss, b_rs)
     tree.start()
 
-    scaled_local = (hidden * own_gain).astype(BF16)
-
-    def project(i, carry):
-        for own, col in ((True, c * 1024 + i * 256), (False, (1 - c) * 1024 + i * 256)):
-            value = mm(scaled_local, wkv[:, pl.ds(pl.multiple_of(col, 256), 256)])
-            if own:
-                d_own[2 * i] = value[:, :128]
-                d_own[2 * i + 1] = value[:, 128:]
-            else:
-                d0_send[2 * i] = value[:, :128].astype(BF16)
-                d0_send[2 * i + 1] = value[:, 128:].astype(BF16)
-        return carry
-
-    lax.fori_loop(0, 4, project, 0)
-    links.send(d0_send, d0_recv, d_ss.at[0], d_rs.at[0], p.partner)
-
-    def consume(core, k):
-        def body(j, carry):
-            tid = p.tid(p.ysrc(k), lax.rem(p.x + j, 4), core)
-            block = full[tid].astype(F32)
-            low, high = block[:, :128], block[:, 128:]
-            ssq[...] += low * low + high * high
-            scaled = jnp.concatenate(
-                [low * gain[pl.ds(2 * tid, 1), :], high * gain[pl.ds(2 * tid + 1, 1), :]], axis=1
-            ).astype(BF16)
-            acc[...] += mm(scaled, wq[pl.ds(pl.multiple_of(tid * PART, PART), PART), :])
-            return carry
-
-        lax.fori_loop(0, 4, body, 0)
-
+    def scaled(tid):
+        block = full[tid].astype(F32)
+        low, high = block[:, :128], block[:, 128:]
+        value = jnp.concatenate([low * gain[pl.ds(2 * tid, 1), :], high * gain[pl.ds(2 * tid + 1, 1), :]], axis=1)
+        return value.astype(BF16), low * low + high * high
+
+    def consume(*items):
+        total, squares = None, None
+        for core, k, shifts in items:
+            for shift in shifts:
+                tid = p.tid(p.ysrc(k), p.xat(shift), core)
+                value, square = scaled(tid)
+                part = mm(value, wq[pl.ds(pl.multiple_of(tid * PART, PART), PART), :])
+                total = part if total is None else total + part
+                squares = square if squares is None else squares + square
+        ssq[...] += squares
+        acc[...] += total
+
+    near, far = (0, 1, 3), (2,)
+    tree.step_x(0)
     tree.step_y(1)
-    tree.step_x(0)
-    links.wait(d0_recv, d_ss.at[0], d_rs.at[0], p.partner)
-    for i in range(4):
-        g = 2 * i + 1 - p.pair
-        d1_send[i] = (d_own[g] + d0_recv[g].astype(F32)).astype(BF16)
-    links.send(d1_send, d1_recv, d_ss.at[1], d_rs.at[1], p.mirror)
+    tree.partner_near(0)
+    links.wait(w_far.at[0], d_ss.at[0], d_rs.at[0], p.partner)
+    links.wait(w_far.at[1], d_ss.at[1], d_rs.at[1], p.mirror)
+    links.wait(w_far.at[2], d_ss.at[7], d_rs.at[7], p.mirror_other)
+    weights_of = ((t, w_own.at[c, p.pair]), (p.partner, w_far.at[0]), (p.mirror, w_far.at[1]), (p.mirror_other, w_far.at[2]))
+    low_sum, high_sum = jnp.zeros((ROWS, 256), F32), jnp.zeros((ROWS, 256), F32)
+    for tid, ref in weights_of:
+        value = scaled(tid)[0]
+        low_sum = low_sum + mm(value, ref[:, :256])
+        high_sum = high_sum + mm(value, ref[:, 256:])
+    for i, value in enumerate((low_sum, high_sum)):
+        d_own[2 * i] = value[:, :128]
+        d_own[2 * i + 1] = value[:, 128:]
+    for k in (1, 2, 3):
+        d2_send[k] = d_own[p.ydst(k)].astype(BF16)
+        links.send(d2_send.at[k], d2_recv.at[k], d_ss.at[1 + k], d_rs.at[1 + k], p.tid(p.ydst(k), p.x, c))
     tree.step_y(2)
     tree.step_x(1)
+    tree.step_y(3)
     tree.step_far(0)
-    consume(c, 0)
-    links.wait(d1_recv, d_ss.at[1], d_rs.at[1], p.mirror)
-
-    def pair_sum(i):
-        g = 2 * i + p.pair
-        return d_own[g] + d0_recv[g].astype(F32) + d1_recv[i].astype(F32)
-
-    for k in (1, 2, 3):
-        d2_send[k] = pair_sum(p.ydst(k)).astype(BF16)
-        links.send(d2_send.at[k], d2_recv.at[k], d_ss.at[1 + k], d_rs.at[1 + k], p.tid(p.ydst(k), p.x, c))
-    tree.step_y(3)
+    consume((c, 0, near), (1 - c, 0, near))
     tree.step_x(2)
     tree.step_far(1)
-    consume(c, 1)
-    column = pair_sum(p.y)
+    consume((c, 1, near))
+    tree.partner_near(1)
+    column = d_own[p.y]
     for k in (1, 2, 3):
         links.wait(d2_recv.at[k], d_ss.at[1 + k], d_rs.at[1 + k], p.tid(p.ysrc(k), p.x, c))
         column = column + d2_recv[k].astype(F32)
     d3_send[...] = column.astype(BF16)
     links.send(d3_send, d3_recv, d_ss.at[5], d_rs.at[5], p.mate)
+    consume((1 - c, 1, near))
     tree.step_x(3)
     tree.step_far(2)
-    tree.step_partner(0)
-    consume(1 - c, 0)
-    consume(c, 2)
+    consume((c, 2, near), (c, 0, far))
     links.wait(d3_recv, d_ss.at[5], d_rs.at[5], p.mate)
     kvraw[c] = column + d3_recv[...].astype(F32)
     links.send(kvraw.at[c], kvraw.at[c], d_ss.at[6], d_rs.at[6], p.partner)
-    tree.step_partner(1)
-    consume(1 - c, 1)
+    tree.partner_near(2)
+    tree.partner_far(0)
+    consume((1 - c, 2, near), (1 - c, 0, far))
+    consume((c, 3, near), (c, 1, far))
+    tree.partner_near(3)
     tree.step_far(3)
-    consume(c, 3)
-    tree.step_partner(2)
-    consume(1 - c, 2)
-    tree.step_partner(3)
-    consume(1 - c, 3)
+    tree.partner_far(1)
+    tree.partner_far(2)
+    consume((1 - c, 3, near), (1 - c, 1, far))
+    consume((c, 2, far), (c, 3, far), (1 - c, 2, far))
+    tree.partner_far(3)
+    consume((1 - c, 3, far))
     links.wait(kvraw.at[1 - c], d_ss.at[6], d_rs.at[6], p.partner)
 
     cosine, sine = cos_s[...], sin_s[...]
@@ -382,7 +410,7 @@
     attended = mm(low, value).astype(BF16)
     att[:, :128] = attended[:ROWS]
     att[:, 128:] = attended[ROWS:]
-    att_copy = pltpu.make_async_copy(att, att_out, local_sem.at[11])
+    att_copy = pltpu.make_async_copy(att, att_out, local_sem.at[10])
     att_copy.start()
     weight_grad = mm_nt(upstream, value)
     inner = jnp.sum(weights * weight_grad, axis=1, keepdims=True)
@@ -390,8 +418,7 @@
     kv_f32[0] = mm_tn(score_grad, query)
     kv_f32[1] = mm_tn(low, upstream)
     e1_send[...] = kv_f32[...].astype(BF16)
-    other = pl.multiple_of((1 - c) * HALF, HALF)
-    links.send(e1_send.at[:, pl.ds(other, HALF), :], e1_recv, g_ss.at[0], g_rs.at[0], p.partner)
+    links.send(e1_send.at[1 - c], e1_recv, e_ss.at[0], e_rs.at[0], p.partner)
     query_grad = mm(score_grad, key)
     for h in (0, 1):
         piece = unrotate(query_grad[h * ROWS : h * ROWS + ROWS], cosine, sine, sign).astype(BF16)
@@ -403,34 +430,44 @@
             rs_rows[pl.ds(0, ROWS), :] += product
     rs_rows[pl.ds(ROWS, 64), :] = jnp.zeros((64, 128), F32)
 
+    def products(k):
+        rows = pl.ds(pl.multiple_of(p.ydst(k) * (8 * PART), 8 * PART), 8 * PART)
+        products_s[k] = mm_nt(q_grad[...], wq[rows, :])
+
     def partial(k, shift, core):
-        tid = p.tid(p.ydst(k), lax.rem(p.x + shift, 4), core)
-        return mm_nt(q_grad[...], wq[pl.ds(pl.multiple_of(tid * PART, PART), PART), :])
-
-    def f_cores(k):
-        def body(j, carry):
-            f0_send[k, j] = partial(k, j, 1 - c).astype(BF16)
-            return carry
-
-        lax.fori_loop(0, 4, body, 0)
-        links.send(f0_send.at[k], f0_recv.at[k], f_ss.at[k], f_rs.at[k], p.partner)
+        col = (lax.rem(p.x + shift, 4) * 2 + core) * PART
+        return products_s[k, :, pl.ds(pl.multiple_of(col, PART), PART)]
+
+    def f_cores(k, which=(2, 1, 3, 0)):
+        for j in which:
+            value = partial(k, j, 1 - c)
+            if k == 0:
+                value = value + kv_part[j, 1]
+            f0_send[k, j] = value.astype(BF16)
+            links.send(f0_send.at[k, j], f0_recv.at[k, j], c_ss.at[4 * k + j], c_rs.at[4 * k + j], p.partner)
 
     top, bottom = pl.ds(0, HALF), pl.ds(HALF, HALF)
 
-    def f_first(k):
-        links.wait(f0_recv.at[k], f_ss.at[k], f_rs.at[k], p.partner)
-        far_send[k] = (partial(k, 2, c) + f0_recv[k, 2].astype(F32)).astype(BF16)
+    def chip_sum(k, shift):
+        links.wait(f0_recv.at[k, shift], c_ss.at[4 * k + shift], c_rs.at[4 * k + shift], p.partner)
+        value = partial(k, shift, c) + f0_recv[k, shift].astype(F32)
+        return value + kv_part[shift, 0] if k == 0 else value
+
+    def f_far(k):
+        far_send[k] = chip_sum(k, 2).astype(BF16)
         links.send(far_send.at[k, top], far_l.at[k], f_ss.at[4 + k], f_rs.at[4 + k], p.right)
         links.send(far_send.at[k, bottom], far_r.at[k], f_ss.at[8 + k], f_rs.at[8 + k], p.left)
-        value = partial(k, 1, c) + f0_recv[k, 1].astype(F32)
+
+    def f_direct(k):
+        value = chip_sum(k, 1)
         r_send[k, bottom] = value[HALF:].astype(BF16)
         links.send(r_send.at[k, bottom], from_l.at[k, bottom], f_ss.at[12 + k], f_rs.at[12 + k], p.right)
         s_r[k] = value[:HALF]
-        value = partial(k, 3, c) + f0_recv[k, 3].astype(F32)
+        value = chip_sum(k, 3)
         l_send[k, top] = value[:HALF].astype(BF16)
         links.send(l_send.at[k, top], from_r.at[k, top], f_ss.at[16 + k], f_rs.at[16 + k], p.left)
         s_l[k] = value[HALF:]
-        s_own[k] = partial(k, 0, c) + f0_recv[k, 0].astype(F32)
+        s_own[k] = chip_sum(k, 0)
 
     def f_second(k):
         links.wait(far_l.at[k], f_ss.at[4 + k], f_rs.at[4 + k], p.left)
@@ -454,70 +491,69 @@
                 y_send.at[k], y_recv.at[k], f_ss.at[28 + k], f_rs.at[28 + k], p.tid(p.ydst(k), p.x, c)
             )
 
-    grads = Tree(links, p, ebuf, 64, e_ss, e_rs)
+    products(1)
     f_cores(1)
+    links.wait(e1_recv, e_ss.at[0], e_rs.at[0], p.partner)
+    chip_grad = kv_f32[c] + e1_recv[...].astype(F32)
+    e2_send[...] = chip_grad.astype(BF16)
+    links.send(e2_send, e2_recv, e_ss.at[1], e_rs.at[1], p.mate)
+    products(2)
+    f_far(1)
     f_cores(2)
-    links.wait(e1_recv, g_ss.at[0], g_rs.at[0], p.partner)
-    mine_rows = pl.ds(pl.multiple_of(c * HALF, HALF), HALF)
-    e_sum[...] = kv_f32[:, mine_rows, :] + e1_recv[...].astype(F32)
-    e2_send[...] = e_sum[...].astype(BF16)
-    links.send(e2_send.at[1 - p.kind], e2_recv, g_ss.at[1], g_rs.at[1], p.mate)
-    f_first(1)
-    f_cores(3)
-    f_first(2)
-    links.wait(e2_recv, g_ss.at[1], g_rs.at[1], p.mate)
-    value_side = p.kind.astype(F32)
-    half_sign = sign[:HALF]
+    f_direct(1)
+    f_far(2)
+    links.wait(e2_recv, e_ss.at[1], e_rs.at[1], p.mate)
+    value_side = c.astype(F32)
     finished = unrotate(
-        e_sum[p.kind] + e2_recv[...].astype(F32),
-        cos_s[mine_rows, :] * (1.0 - value_side) + value_side,
-        sin_s[mine_rows, :] * (1.0 - value_side),
-        half_sign,
+        kv_f32[c] + e1_recv[...].astype(F32) + e2_recv[...].astype(F32),
+        cosine * (1.0 - value_side) + value_side,
+        sine * (1.0 - value_side),
+        sign,
     ).astype(BF16)
-    rs_rows[mine_rows, :] += finished.astype(F32) * kvraw[p.kind, mine_rows, :]
+    rs_rows[pl.ds(0, ROWS), :] += 0.5 * finished.astype(F32) * kvraw[c]
     ones = jnp.ones((8, 128), F32)
     stat = jnp.concatenate([exact_nt(ones, rs_rows[0:128, :]), exact_nt(ones, rs_rows[128:256, :])], axis=0)
     coarse = stat.astype(BF16).astype(F32)
-    ebuf[t, pl.ds(0, HALF)] = finished
-    ebuf[t, pl.ds(HALF, 16)] = jnp.where(lax.rem(iota((16, 128), 0), 2) == 0, coarse, stat - coarse).astype(BF16)
-    grads.start()
-    f_cores(0)
+    ebuf[p.y, pl.ds(0, ROWS)] = finished
+    ebuf[p.y, pl.ds(ROWS, 16)] = jnp.where(lax.rem(iota((16, 128), 0), 2) == 0, coarse, stat - coarse).astype(BF16)
+    for k in (1, 2, 3):
+        links.send(ebuf.at[p.y], ebuf.at[p.y], e_ss.at[1 + k], e_rs.at[1 + k], p.tid(p.ydst(k), p.x, c))
+    f_direct(2)
     f_second(1)
-    f_first(3)
+    products(3)
+    f_cores(3)
+    f_far(3)
     f_second(2)
+    products(0)
+    f_cores(0, (2,))
+    f_direct(3)
     f_third(1)
-    grads.step_y(1)
-    f_first(0)
+    f_far(0)
     f_second(3)
+    for k in (1, 2, 3):
+        links.wait(ebuf.at[p.ysrc(k)], e_ss.at[1 + k], e_rs.at[1 + k], p.tid(p.ysrc(k), p.x, c))
+    mirror_shift = 3 - 2 * p.kind
+    pair_grads = jnp.concatenate([ebuf[i, pl.ds(0, ROWS)] for i in range(4)], axis=1)
+    for (tid, ref), shift, core in zip(weights_of, (0, 0, lax.rem(mirror_shift + 4, 4), lax.rem(mirror_shift + 4, 4)), (0, 1, 0, 1)):
+        kv_part[shift, core] = mm_nt(pair_grads, ref[...])
+    f_cores(0, (1, 3, 0))
+    row_sum = jnp.zeros((16, 128), F32)
+    for i in range(4):
+        row_sum = row_sum + ebuf[i, pl.ds(ROWS, 16)].astype(F32)
+    rs_all[p.row_index] = row_sum
+    for j in range(1, 8):
+        own_row = rs_all.at[p.row_index]
+        links.send(own_row, own_row, r_ss.at[j], r_rs.at[j], p.in_row(j))
     f_third(2)
-    grads.step_y(2)
-    grads.step_x(0)
+    f_direct(0)
+    f_third(3)
     f_second(0)
-    grads.step_y(3)
-    grads.step_x(1)
-    grads.step_far(0)
-    f_third(3)
-    grads.step_x(2)
-    grads.step_far(1)
-    grads.step_x(3)
-    grads.step_far(2)
-    grads.step_far(3)
-    f_third(0)
-    for k in range(4):
-        grads.step_partner(k)
-
-    def place_grad(tid, carry):
-        core = lax.rem(tid, 2)
-        xs = lax.rem(lax.div(tid, 2), 4)
-        ys = lax.div(tid, 8)
-        col = lax.rem(xs, 2) * 1024 + (ys * 2 + lax.div(xs, 2)) * 128
-        kvfull[pl.ds(pl.multiple_of(core * HALF, HALF), HALF), pl.ds(pl.multiple_of(col, 128), 128)] = ebuf[
-            tid, pl.ds(0, HALF)
-        ]
-        return carry + ebuf[tid, pl.ds(HALF, 16)].astype(F32)
-
-    stats = lax.fori_loop(0, LANES, place_grad, jnp.zeros((16, 128), F32))
-    key_value_part = mm_nt(kvfull[...], wkv[...])
+    for j in range(1, 8):
+        back = lax.rem(p.row_index + 8 - j, 8)
+        links.wait(rs_all.at[back], r_ss.at[j], r_rs.at[j], p.y * 8 + back)
+    stats = rs_all[0]
+    for j in range(1, 8):
+        stats = stats + rs_all[j]
     eye = iota((128, 128), 0) == iota((128, 128), 1)
 
     def upright(row):
@@ -526,7 +562,8 @@
     row_stat = jnp.concatenate(
         [upright(stats[0:1] + stats[1:2]), upright(stats[8:9] + stats[9:10])[: ROWS - 128]], axis=0
     ) * (1.0 / D)
-    normed_grad = s_own[0] + key_value_part
+    f_third(0)
+    normed_grad = s_own[0]
     for k in (1, 2, 3):
         links.wait(y_recv.at[k], f_ss.at[28 + k], f_rs.at[28 + k], p.tid(p.ysrc(k), p.x, c))
         normed_grad = normed_grad + y_recv[k].astype(F32)
@@ -535,12 +572,17 @@
         inverse * (own_gain * normed_grad)
         - full[t].astype(F32) * (inverse * inverse * inverse * row_stat)
     ).astype(BF16)
-    grad_copy = pltpu.make_async_copy(grad, grad_out, local_sem.at[12])
+    grad_copy = pltpu.make_async_copy(grad, grad_out, local_sem.at[11])
     grad_copy.start()
     lax.fori_loop(1, N_DP, drain_rollout, 0)
     links.drain()
     att_copy.wait()
     grad_copy.wait()
+
+
+def hand_over(att_in, grad_in, att_out, grad_out):
+    att_out[...] = att_in[...]
+    grad_out[...] = grad_in[...]
 
 
 def on_device(
@@ -562,20 +604,21 @@
     def dma(n):
         return pltpu.SemaphoreType.DMA((n,))
 
-    scratch = [pltpu.VMEM(one.shape, one.dtype) for one in operands]
+    scratch = [pltpu.VMEM(one.shape, one.dtype) for i, one in enumerate(operands) if i != 6]
     scratch += [v(ROWS, PART), v(ROWS, PART)]
     scratch += [
         v(N_DP, WINDOW, PART), v(N_DP, WINDOW, PART), v(LANES, ROWS, PART), v(ROWS, PART, dtype=F32),
         v(ROWS, 128, dtype=F32),
     ]
     scratch += [
-        v(8, ROWS, 128), v(8, ROWS, 128), v(8, ROWS, 128, dtype=F32), v(4, ROWS, 128), v(4, ROWS, 128),
+        v(2, 2, PART, 512), v(3, PART, 512), v(4, ROWS, 128, dtype=F32),
         v(4, ROWS, 128), v(4, ROWS, 128), v(ROWS, 128), v(ROWS, 128), v(2, ROWS, 128, dtype=F32),
     ]
     scratch += [
         v(ROWS, 128, dtype=F32), v(ROWS, 128, dtype=F32), v(ROWS, PART), v(2, ROWS, 128, dtype=F32),
-        v(2, ROWS, 128), v(2, HALF, 128), v(2, HALF, 128, dtype=F32), v(2, HALF, 128), v(HALF, 128),
-        v(LANES, GRAD_ROWS, 128), v(256, 128, dtype=F32), v(ROWS, 2048),
+        v(2, ROWS, 128), v(ROWS, 128), v(ROWS, 128), v(ROWS, 128),
+        v(4, GRAD_ROWS, 128), v(256, 128, dtype=F32), v(8, 16, 128, dtype=F32), v(4, 2, ROWS, PART, dtype=F32),
+        v(4, ROWS, 8 * PART, dtype=F32),
     ]
     scratch += [
         v(4, 4, ROWS, PART), v(4, 4, ROWS, PART), v(4, ROWS, PART), v(4, HALF, PART), v(4, HALF, PART),
@@ -583,14 +626,14 @@
         v(4, HALF, PART, dtype=F32), v(4, HALF, PART, dtype=F32), v(4, ROWS, PART), v(4, ROWS, PART),
     ]
     scratch += [
-        dma(13), dma(N_DP), dma(N_DP), dma(TREE_SLOTS), dma(TREE_SLOTS), dma(7), dma(7),
-        dma(TREE_SLOTS), dma(TREE_SLOTS), dma(2), dma(2), dma(32), dma(32),
+        dma(28), dma(N_DP), dma(N_DP), dma(TREE_SLOTS), dma(TREE_SLOTS), dma(8), dma(8),
+        dma(5), dma(5), dma(8), dma(8), dma(16), dma(16), dma(32), dma(32),
     ]
     shape = jax.ShapeDtypeStruct((ROWS, PART), BF16)
-    return pl.pallas_call(
+    outs = pl.pallas_call(
         kernel,
         out_shape=(shape, shape),
-        in_specs=[pl.BlockSpec(memory_space=pl.ANY)] * len(operands),
+        in_specs=[pl.BlockSpec(memory_space=pltpu.HBM)] * len(operands),
         out_specs=[pl.BlockSpec(memory_space=pl.ANY)] * 2,
         scratch_shapes=scratch,
         compiler_params=pltpu.CompilerParams(
@@ -598,6 +641,7 @@
         ),
         name="step",
     )(*operands)
+    return pl.pallas_call(hand_over, out_shape=(shape, shape), name="hand_over")(*outs)
 
 
 def solution(mesh):

time: 92.2 us -> 80.6 us (0.87)
  Pallas kernels: 88.3 us -> 79.5 us
  local copies, waits for them, and re-layouts: 3.08 us -> 0 us
    pallas_call x1, Pallas kernels: 88.3 us -> 77.9 us  [on_device(): pl.pallas_call(kernel, out_shape=(shape, shape), in_specs=[pl.BlockSpec(m...]
    unnamed x2 -> x0, local copies, waits for them, and re-layouts: 3.08 us -> none
    pallas_call x0 -> x1, Pallas kernels: none -> 1.62 us  [on_device(): pl.pallas_call(hand_over, out_shape=(shape, shape), name='hand_over')(*outs)]
where the time goes in v2:
time: 80.6 us; the launch traced here: 80.2 us
  Pallas kernels  79.5 us (99%)
    pallas_call x1, Pallas kernels, on_device(): pl.pallas_call(kernel, out_shape=(shape, shape), in_specs=[pl.BlockSpec(m...  77.9 us
    pallas_call x1, Pallas kernels, on_device(): pl.pallas_call(hand_over, out_shape=(shape, shape), name='hand_over')(*outs)  1.62 us

profile of v2, /device:TPU:1, one launch (start us, length us, event | category | flops | bytes accessed | tf_op | source)
XLA Modules:
  0.0 80.2 jit_solution(4839182358056265761)
XLA Ops:
  0.6 77.9 %step.1 = (bf16[192,256]{1,0:T(8,128)(2,1)}, bf16[192,256]{1,0:T(8,128)(2,1)}) custom-call(bf16[24,16,256]{2,1,0:T(8,128)(2,1)} %slots_in.1, s32[24,24]{1,0:T(8,128)} %lengths_in.1, s32[24,24]{1,0:T(8,128)} %owners_in.1, f32[64,128]{1,0:T(8,128)} %bitcast.3, bf16[8192,256]{1,0:T(8,128)(2,1)} %wq_in.1, f32[2,128]{1,0:T(2,128)} %bitcast.5, ...), custom_call_target="tpu_custom_call" | custom-call | tf_op jit(solution)/shard_map/step/pallas_call | solution.py:633
  78.6 1.6 %hand_over.1 = (bf16[192,256]{1,0:T(8,128)(2,1)}, bf16[192,256]{1,0:T(8,128)(2,1)}) custom-call(bf16[192,256]{1,0:T(8,128)(2,1)} %get-tuple-element.4.att_in, bf16[192,256]{1,0:T(8,128)(2,1)} %get-tuple-element.5.grad_in), custom_call_target="tpu_custom_call" | custom-call | tf_op jit(solution)/shard_map/hand_over/pallas_call | solution.py:644

commit v3 on v2

v3 whole, which is shorter than its diff:
```python
import jax
import jax.numpy as jnp
import numpy as np
from jax import lax
from jax.experimental import pallas as pl
from jax.experimental.pallas import tpu as pltpu
from jax.sharding import PartitionSpec as P

D = 8192
HEADS = 64
KV_HEADS = 8
HEAD_DIM = 128
EPSILON = 1e-06
ROPE_BASE = 1000000.0
N_DP = 24
WINDOW = 16
ROWS = 192
HALF = 96
PART = 256
LANES = 32
HALF_DIM = HEAD_DIM // 2
SCALE = HEAD_DIM ** (-0.5)
MESH = pl.DeviceIdType.MESH
F32 = jnp.float32
BF16 = jnp.bfloat16
TREE_SLOTS = 23
GRAD_ROWS = ROWS + 16
ORDER = (1, 2, 3, 0)


def mm(a, b):
    return jnp.dot(a, b, preferred_element_type=F32)


def mm_nt(a, b):
    return lax.dot_general(a, b, (((1,), (1,)), ((), ())), preferred_element_type=F32)


def mm_tn(a, b):
    return lax.dot_general(a, b, (((0,), (0,)), ((), ())), preferred_element_type=F32)


def exact_nt(a, b):
    return lax.dot_general(
        a, b, (((1,), (1,)), ((), ())), preferred_element_type=F32, precision=lax.Precision.HIGHEST
    )


def exact_mm(a, b):
    return lax.dot_general(
        a, b, (((1,), (0,)), ((), ())), preferred_element_type=F32, precision=lax.Precision.HIGHEST
    )


def iota(shape, dim):
    return lax.broadcasted_iota(jnp.int32, shape, dim)


class Links:
    def __init__(self, dp):
        self.dp = dp

    def copy(self, src, dst, send_sem, recv_sem, peer):
        return pltpu.make_async_remote_copy(
            src_ref=src,
            dst_ref=dst,
            send_sem=send_sem,
            recv_sem=recv_sem,
            device_id=(self.dp, peer),
            device_id_type=MESH,
        )

    def send(self, src, dst, send_sem, recv_sem, peer):
        self.copy(src, dst, send_sem, recv_sem, peer).start()

    def wait(self, dst, send_sem, recv_sem, peer):
        self.copy(dst, dst, send_sem, recv_sem, peer).wait_recv()

    def sent(self, bytes_of, send_sem, recv_sem, peer):
        self.copy(bytes_of, bytes_of, send_sem, recv_sem, peer).wait_send()


class Tree:
    def __init__(self, links, place, buffer, cuts, send_sem, recv_sems, base):
        self.links = links
        self.place = place
        self.buffer = buffer
        self.small, self.large = cuts
        self.ss = send_sem
        self.rs = recv_sems
        self.base = base

    def block(self, tid):
        return self.buffer.at[tid]

    def send(self, slot, ref, peer):
        self.links.send(ref, ref, self.ss, self.rs.at[self.base + slot], peer)

    def wait(self, slot, ref, peer):
        self.links.wait(ref, self.ss, self.rs.at[self.base + slot], peer)

    def spread(self, k):
        p = self.place
        ref = self.block(p.tid(p.ysrc(k), p.x, p.c))
        self.send(3 + k, ref, p.mate)
        self.send(7 + k, ref, p.mirror)
        self.send(15 + k, ref, p.partner)

    def start(self):
        p = self.place
        ref = self.block(p.t)
        for k in (1, 2):
            self.send(k - 1, ref, p.tid(p.ydst(k), p.x, p.c))
        self.spread(0)

    def step_y(self, k):
        p = self.place
        ref = self.block(p.tid(p.ysrc(k), p.x, p.c))
        self.wait(k - 1, ref, p.tid(p.ysrc(k), p.x, p.c))
        if k == 2:
            self.send(2, ref, p.tid(p.ydst(1), p.x, p.c))
        self.spread(k)

    def step_mate(self, k):
        p = self.place
        tid = p.tid(p.ysrc(k), p.x + 1 - 2 * p.kind, p.c)
        self.wait(3 + k, self.block(tid), p.mate)
        rows = pl.ds(pl.multiple_of((1 - p.kind) * self.large, 16), self.small)
        self.send(11 + k, self.buffer.at[tid, rows], p.mirror)
        self.send(15 + k, self.block(tid), p.partner)

    def step_mirror(self, k):
        p = self.place
        tid = p.tid(p.ysrc(k), 3 - p.x, p.c)
        self.wait(7 + k, self.block(tid), p.mirror)
        rows = pl.ds(pl.multiple_of(p.kind * self.small, 16), self.large)
        self.send(11 + k, self.buffer.at[tid, rows], p.mate)
        self.send(15 + k, self.block(tid), p.partner)

    def step_far(self, k):
        p = self.place
        tid = p.tid(p.ysrc(k), p.xat(2), p.c)
        self.wait(11 + k, self.block(tid), p.left)
        self.send(19 + k, self.block(tid), p.partner)

    def partner_near(self, k):
        self.wait(15 + k, self.buffer.at[pl.ds(0, 3)], self.place.partner)

    def partner_far(self, k):
        p = self.place
        self.wait(19 + k, self.block(p.tid(p.ysrc(k), p.xat(2), 1 - p.c)), p.partner)

    def sent(self):
        self.links.sent(self.buffer.at[pl.ds(0, 31)], self.ss, self.rs.at[self.base], self.place.partner)


class Place:
    def __init__(self):
        self.dp = lax.axis_index("dp")
        self.t = lax.axis_index("tensor")
        self.c = lax.rem(self.t, 2)
        self.x = lax.rem(lax.div(self.t, 2), 4)
        self.y = lax.div(self.t, 8)
        self.left = self.tid(self.y, self.xat(3), self.c)
        self.right = self.tid(self.y, self.xat(1), self.c)
        self.partner = self.tid(self.y, self.x, 1 - self.c)
        self.pair = lax.div(self.x, 2)
        self.kind = lax.rem(self.x, 2)
        self.mirror = self.tid(self.y, 3 - self.x, self.c)
        self.mirror_other = self.tid(self.y, 3 - self.x, 1 - self.c)
        self.row_index = self.x * 2 + self.c
        self.mate = self.tid(self.y, self.x + 1 - 2 * self.kind, self.c)

    def in_row(self, j):
        return self.y * 8 + lax.rem(self.row_index + j, 8)

    def tid(self, y, x, c):
        return (y * 4 + x) * 2 + c

    def xat(self, shift):
        return lax.rem(self.x + shift, 4)

    def ydst(self, k):
        if k == 3:
            return 3 - self.y
        if k == 2:
            return self.y + 2 - 4 * lax.div(self.y, 2)
        if k == 1:
            return self.y + 1 - 2 * lax.rem(self.y, 2)
        return self.y

    def ysrc(self, k):
        return self.ydst(k)


def kernel(
    slots_in, lengths_in, owners_in, gain_in, wq_in, qbias_in, wkv_in, kvbias_in, up_in, cos_in, sin_in,
    att_out, grad_out,
    slots, lengths, owners, gain, wq, qbias, kvbias, up, cos16, sin16, att, grad,
    owner_table, a_send, a_recv, full_low, full_high, acc, ssq,
    w_own, w_far, d_own, d2_send, d2_recv, d3_send, d3_recv, kvraw,
    cos_s, sin_s, q_grad, kv_f32, e1_send, e1_recv, e2_send, e2_recv, ebuf, rs_rows, rs_all, products_s,
    f0_send, f0_recv, far_send, from_mate, from_mirror, mate_send, mirror_send, column_in, s_own, s_mate, s_mirror, y_send, y_recv,
    local_sem, a_ss, a_rs, b_ss, b_rs, d_ss, d_rs, e_ss, e_rs, f_ss, f_rs,
):
    p = Place()
    dp, t, c = p.dp, p.t, p.c

    pairs = (
        (owners_in, owner_table), (slots_in, slots), (owners_in, owners), (lengths_in, lengths), (gain_in, gain),
        (kvbias_in, kvbias), (qbias_in, qbias), (cos_in, cos16), (sin_in, sin16), (up_in, up), (wq_in, wq),
    )
    loads = [pltpu.make_async_copy(a, b, local_sem.at[i]) for i, (a, b) in enumerate(pairs)]
    weight_loads = []
    for kind in (0, 1):
        for pair in (0, 1):
            for i in range(4):
                weight_loads.append(
                    pltpu.make_async_copy(
                        wkv_in.at[:, pl.ds(kind * 1024 + (2 * i + pair) * 128, 128)],
                        w_own.at[kind, pair, :, pl.ds(i * 128, 128)],
                        local_sem.at[12],
                    )
                )
    for one in loads[:2]:
        one.start()

    barrier = pltpu.get_barrier_semaphore()

    def greet(k, carry):
        pl.semaphore_signal(barrier, inc=1, device_id=(lax.rem(dp + k, N_DP), t), device_id_type=MESH)
        return carry

    lax.fori_loop(1, N_DP, greet, 0)
    for peer in tuple(p.in_row(j) for j in range(1, 8)) + tuple(p.tid(p.ydst(k), p.x, c) for k in (1, 2, 3)):
        pl.semaphore_signal(barrier, inc=1, device_id=(dp, peer), device_id_type=MESH)

    for one in loads[2:] + weight_loads:
        one.start()

    total = N_DP * WINDOW
    loads[0].wait()
    slot_of = []
    for b in range(N_DP):
        found = jnp.int32(0)
        for j in range(1, N_DP):
            found = jnp.where(owner_table[b, j] == dp, j, found)
        slot_of.append(found)
    loads[1].wait()
    for b in range(N_DP):
        block = slots[slot_of[b]]
        for h in (0, 1):
            a_send[h, b] = block[:, h * 128 : h * 128 + 128]
    for h in (0, 1):
        a_recv[h, dp] = a_send[h, dp]
    pl.semaphore_wait(barrier, N_DP - 1 + 10)

    def rollout(src, dst, k, peer):
        return pltpu.make_async_remote_copy(
            src_ref=src, dst_ref=dst, send_sem=a_ss.at[0], recv_sem=a_rs.at[k], device_id=(peer, t), device_id_type=MESH
        )

    def send_rollout(i, carry):
        h, k = lax.div(i, N_DP - 1), lax.rem(i, N_DP - 1) + 1
        peer = lax.rem(dp + k, N_DP)
        rollout(a_send.at[h, peer], a_recv.at[h, dp], h, peer).start()
        return carry

    def wait_rollout(h):
        most = a_recv.at[h, pl.ds(0, N_DP - 1)]
        rollout(most, most, h, lax.rem(dp + 1, N_DP)).wait_recv()

    lax.fori_loop(0, 2 * (N_DP - 1), send_rollout, 0)

    pltpu.make_async_copy(w_own, w_own, local_sem.at[12]).wait()
    for one in loads[2:]:
        one.wait()
    links = Links(dp)
    links.send(w_own.at[1 - c, p.pair], w_far.at[0], d_ss.at[0], d_rs.at[0], p.partner)
    links.send(w_own.at[c, 1 - p.pair], w_far.at[1], d_ss.at[0], d_rs.at[0], p.mirror)
    links.send(w_own.at[1 - c, 1 - p.pair], w_far.at[2], d_ss.at[0], d_rs.at[0], p.mirror_other)

    length_row = jnp.broadcast_to(lengths[pl.ds(dp, 1), :].astype(F32), (ROWS, N_DP))
    owner_row = jnp.broadcast_to(owners[pl.ds(dp, 1), :].astype(F32), (ROWS, N_DP))
    before = (iota((N_DP, N_DP), 0) < iota((N_DP, N_DP), 1)).astype(F32).astype(BF16)
    starts = mm(length_row.astype(BF16), before)
    place = iota((ROWS, N_DP), 0).astype(F32)
    inside = (place >= starts) & (place < starts + length_row)
    start = jnp.sum(jnp.where(inside, starts, 0.0), axis=1, keepdims=True)
    source = jnp.sum(jnp.where(inside, owner_row, 0.0), axis=1, keepdims=True)
    offset = iota((ROWS, 1), 0).astype(F32) - start
    wanted = (source * WINDOW + offset).astype(jnp.int32)
    select = (iota((ROWS, total), 1) == wanted).astype(F32).astype(BF16)
    turn = (iota((ROWS, WINDOW), 1) == offset.astype(jnp.int32)).astype(F32)
    sign = jnp.where(iota((ROWS, HEAD_DIM), 1) < HALF_DIM, -1.0, 1.0)
    cos_s[...] = exact_mm(turn, cos16[...])
    sin_s[...] = exact_mm(turn, sin16[...])
    key_place = iota((ROWS, ROWS), 1)
    allowed = (key_place >= start.astype(jnp.int32)) & (key_place <= iota((ROWS, ROWS), 0))
    acc[...] = jnp.zeros_like(acc)
    ssq[...] = jnp.zeros_like(ssq)
    trees = [
        Tree(links, p, ref, (80, 112), b_ss.at[h], b_rs, h * TREE_SLOTS) for h, ref in enumerate((full_low, full_high))
    ]
    for h, ref in enumerate((full_low, full_high)):
        wait_rollout(h)
        ref[t] = mm(select, a_recv[h].reshape(total, 128)).astype(BF16)
        trees[h].start()

    def steps(name, k):
        for tree in trees:
            getattr(tree, name)(k)

    def scaled(tid):
        low, high = full_low[tid].astype(F32), full_high[tid].astype(F32)
        value = jnp.concatenate([low * gain[pl.ds(2 * tid, 1), :], high * gain[pl.ds(2 * tid + 1, 1), :]], axis=1)
        return value.astype(BF16), low * low + high * high

    def consume(*items):
        total, squares = None, None
        for core, k, shifts in items:
            for shift in shifts:
                tid = p.tid(p.ysrc(k), p.xat(shift), core)
                value, square = scaled(tid)
                part = mm(value, wq[pl.ds(pl.multiple_of(tid * PART, PART), PART), :])
                total = part if total is None else total + part
                squares = square if squares is None else squares + square
        ssq[...] += squares
        acc[...] += total

    near, far = (0, 1, 3), (2,)
    first, second = trees
    first.step_mate(0)
    first.step_y(1)
    first.step_mirror(0)
    first.step_y(2)
    second.step_mate(0)
    second.step_y(1)
    second.step_mirror(0)
    second.step_y(2)
    first.step_mate(1)
    first.step_y(3)
    steps("partner_near", 0)
    links.wait(w_far, d_ss.at[0], d_rs.at[0], p.partner)
    weights_of = ((t, w_own.at[c, p.pair]), (p.partner, w_far.at[0]), (p.mirror, w_far.at[1]), (p.mirror_other, w_far.at[2]))
    low_sum, high_sum = jnp.zeros((ROWS, 256), F32), jnp.zeros((ROWS, 256), F32)
    for tid, ref in weights_of:
        value = scaled(tid)[0]
        low_sum = low_sum + mm(value, ref[:, :256])
        high_sum = high_sum + mm(value, ref[:, 256:])
    for i, value in enumerate((low_sum, high_sum)):
        d_own[2 * i] = value[:, :128]
        d_own[2 * i + 1] = value[:, 128:]
    for k in (1, 2, 3):
        d2_send[k] = d_own[p.ydst(k)].astype(BF16)
        links.send(d2_send.at[k], d2_recv.at[k], d_ss.at[1], d_rs.at[1], p.tid(p.ydst(k), p.x, c))
    first.step_mirror(1)
    second.step_mate(1)
    second.step_y(3)
    second.step_mirror(1)
    steps("step_far", 0)
    consume((c, 0, near), (1 - c, 0, near))
    first.step_mate(2)
    first.step_mirror(2)
    second.step_mate(2)
    second.step_mirror(2)
    steps("step_far", 1)
    consume((c, 1, near))
    column = d_own[p.y]
    links.wait(d2_recv.at[pl.ds(1, 3)], d_ss.at[1], d_rs.at[1], p.mate)
    for k in (1, 2, 3):
        column = column + d2_recv[k].astype(F32)
    d3_send[...] = column.astype(BF16)
    links.send(d3_send, d3_recv, d_ss.at[1], d_rs.at[2], p.mate)
    steps("partner_near", 1)
    consume((1 - c, 1, near))
    steps("step_mate", 3)
    steps("step_mirror", 3)
    steps("step_far", 2)
    consume((c, 2, near), (c, 0, far))
    steps("partner_near", 2)
    steps("partner_far", 0)
    consume((1 - c, 2, near), (1 - c, 0, far))
    consume((c, 3, near))
    steps("step_far", 3)
    links.wait(d3_recv, d_ss.at[1], d_rs.at[2], p.mate)
    kvraw[c] = column + d3_recv[...].astype(F32)
    links.send(kvraw.at[c], kvraw.at[c], d_ss.at[2], d_rs.at[3], p.partner)
    consume((c, 1, far), (c, 2, far), (c, 3, far))
    steps("partner_near", 3)
    steps("partner_far", 1)
    steps("partner_far", 2)
    consume((1 - c, 3, near), (1 - c, 1, far))
    steps("partner_far", 3)
    consume((1 - c, 2, far), (1 - c, 3, far))
    links.wait(kvraw.at[1 - c], d_ss.at[2], d_rs.at[3], p.partner)

    cosine, sine = cos_s[...], sin_s[...]
    inverse = lax.rsqrt(jnp.sum(ssq[...], axis=1, keepdims=True) * (1.0 / D) + EPSILON)

    def rotate(u):
        return u * cosine + pltpu.roll(u, HALF_DIM, 1) * (sign * sine)

    def unrotate(z, cosine, sine, sign):
        return z * cosine - pltpu.roll(z * sine, HALF_DIM, 1) * sign

    group = p.y * 2 + p.pair
    key_raw, value_raw = kvraw[0], kvraw[1]
    key = rotate(inverse * key_raw + kvbias[pl.ds(group, 1), :]).astype(BF16)
    value = (inverse * value_raw + kvbias[pl.ds(KV_HEADS + group, 1), :]).astype(BF16)
    query = jnp.concatenate(
        [rotate(inverse * acc[:, h * 128 : h * 128 + 128] + qbias[h : h + 1, :]).astype(BF16) for h in (0, 1)], axis=0
    )
    upstream = jnp.concatenate([up[:, :128], up[:, 128:]], axis=0)
    both = jnp.concatenate([allowed.astype(F32), allowed.astype(F32)], axis=0) > 0.5
    scores = jnp.where(both, mm_nt(query, key) * SCALE, -1e30)
    highest = jnp.max(scores, axis=1, keepdims=True)
    exponent = jnp.where(both, jnp.exp(scores - highest), 0.0)
    weights = exponent / jnp.sum(exponent, axis=1, keepdims=True)
    low = weights.astype(BF16)
    weight_grad = mm_nt(upstream, value)
    inner = jnp.sum(weights * weight_grad, axis=1, keepdims=True)
    score_grad = (weights * (weight_grad - inner) * SCALE).astype(BF16)
    query_grad = mm(score_grad, key)
    for h in (0, 1):
        piece = unrotate(query_grad[h * ROWS : h * ROWS + ROWS], cosine, sine, sign).astype(BF16)
        q_grad[:, h * 128 : h * 128 + 128] = piece

    def products(k):
        rows = pl.ds(pl.multiple_of(p.ydst(k) * (8 * PART), 8 * PART), 8 * PART)
        products_s[k] = mm_nt(q_grad[...], wq[rows, :])

    def partial(k, shift, core):
        col = (lax.rem(p.x + shift, 4) * 2 + core) * PART
        return products_s[k, :, pl.ds(pl.multiple_of(col, PART), PART)]

    kind = p.kind
    far_shift, mate_shift, mirror_shift = 2, 1 + 2 * kind, 3 - 2 * kind

    def rows_of(index):
        return pl.ds(pl.multiple_of(index * HALF, HALF), HALF)

    def f_core(k, shift, sem, more=None):
        value = partial(k, shift, 1 - c)
        if more is not None:
            value = value + more
        f0_send[k, shift] = value.astype(BF16)
        links.send(f0_send.at[k, shift], f0_recv.at[k, shift], f_ss.at[0], f_rs.at[sem], p.partner)

    def f_cores_far(k):
        f_core(k, far_shift, k)

    def f_cores_mate(k):
        f_core(k, mate_shift, 4 + k)

    def f_cores_rest(k):
        f_core(k, mirror_shift, 8 + k)
        f_core(k, 0, 8 + k)

    def chip_sum(k, shift):
        return partial(k, shift, c) + f0_recv[k, shift].astype(F32)

    def f_far(k):
        links.wait(f0_recv.at[k, 2], f_ss.at[0], f_rs.at[k], p.partner)
        far_send[k] = chip_sum(k, far_shift).astype(BF16)
        links.send(far_send.at[k, rows_of(kind)], from_mate.at[k], f_ss.at[1], f_rs.at[12 + k], p.mate)
        links.send(far_send.at[k, rows_of(1 - kind)], from_mirror.at[k], f_ss.at[1], f_rs.at[16 + k], p.mirror)

    def f_mate(k):
        links.wait(f0_recv.at[k, 1], f_ss.at[0], f_rs.at[4 + k], p.partner)
        s_mate[k] = chip_sum(k, mate_shift)
        mate_send[k, rows_of(1 - kind)] = s_mate[k, rows_of(1 - kind)].astype(BF16)
        one = mate_send.at[k, rows_of(1 - kind)]
        links.send(one, column_in.at[k, 0, rows_of(1 - kind)], f_ss.at[1], f_rs.at[20 + k], p.mate)

    def f_rest(k, mirror_more=None, own_more=None):
        links.wait(f0_recv.at[k, pl.ds(0, 2)], f_ss.at[0], f_rs.at[8 + k], p.partner)
        value = chip_sum(k, mirror_shift)
        s_mirror[k] = value if mirror_more is None else value + mirror_more
        mirror_send[k, rows_of(kind)] = s_mirror[k, rows_of(kind)].astype(BF16)
        one = mirror_send.at[k, rows_of(kind)]
        links.send(one, column_in.at[k, 1, rows_of(kind)], f_ss.at[1], f_rs.at[20 + k], p.mirror)
        value = chip_sum(k, 0)
        s_own[k] = value if own_more is None else value + own_more

    def f_relay_mate(k):
        links.wait(from_mirror.at[k], f_ss.at[1], f_rs.at[16 + k], p.mirror)
        mate_send[k, rows_of(kind)] = (s_mate[k, rows_of(kind)] + from_mirror[k].astype(F32)).astype(BF16)
        one = mate_send.at[k, rows_of(kind)]
        links.send(one, column_in.at[k, 0, rows_of(kind)], f_ss.at[1], f_rs.at[20 + k], p.mate)

    def f_relay_mirror(k):
        links.wait(from_mate.at[k], f_ss.at[1], f_rs.at[12 + k], p.mate)
        mirror_send[k, rows_of(1 - kind)] = (s_mirror[k, rows_of(1 - kind)] + from_mate[k].astype(F32)).astype(BF16)
        one = mirror_send.at[k, rows_of(1 - kind)]
        links.send(one, column_in.at[k, 1, rows_of(1 - kind)], f_ss.at[1], f_rs.at[20 + k], p.mirror)

    def f_third(k):
        links.wait(column_in.at[k], f_ss.at[1], f_rs.at[20 + k], p.mate)
        value = s_own[k] + column_in[k, 0].astype(F32) + column_in[k, 1].astype(F32)
        if k == 0:
            s_own[k] = value
        else:
            if k == 2:
                links.wait(y_recv.at[3], f_ss.at[2], f_rs.at[26], p.tid(p.ydst(1), p.x, c))
                value = value + y_recv[3].astype(F32)
            y_send[k] = value.astype(BF16)
            peer = p.tid(p.ydst(2 if k == 2 else 1), p.x, c)
            links.send(y_send.at[k], y_recv.at[k], f_ss.at[2], f_rs.at[23 + k], peer)

    products(3)
    f_cores_far(3)
    kv_f32[0] = mm_tn(score_grad, query)
    kv_f32[1] = mm_tn(low, upstream)
    e1_send[...] = kv_f32[...].astype(BF16)
    links.send(e1_send.at[1 - c], e1_recv, e_ss.at[0], e_rs.at[0], p.partner)
    f_cores_mate(3)
    f_cores_rest(3)
    attended = mm(low, value).astype(BF16)
    att[:, :128] = attended[:ROWS]
    att[:, 128:] = attended[ROWS:]
    att_copy = pltpu.make_async_copy(att, att_out, local_sem.at[13])
    att_copy.start()
    for h in (0, 1):
        inner_part = q_grad[:, h * 128 : h * 128 + 128].astype(F32) * acc[:, h * 128 : h * 128 + 128]
        if h == 0:
            rs_rows[pl.ds(0, ROWS), :] = inner_part
        else:
            rs_rows[pl.ds(0, ROWS), :] += inner_part
    rs_rows[pl.ds(ROWS, 64), :] = jnp.zeros((64, 128), F32)
    f_far(3)
    links.wait(e1_recv, e_ss.at[0], e_rs.at[0], p.partner)
    chip_grad = kv_f32[c] + e1_recv[...].astype(F32)
    e2_send[...] = chip_grad.astype(BF16)
    links.send(e2_send, e2_recv, e_ss.at[0], e_rs.at[1], p.mate)
    f_mate(3)
    products(2)
    f_cores_far(2)
    f_cores_mate(2)
    f_cores_rest(2)
    f_rest(3)
    f_far(2)
    links.wait(e2_recv, e_ss.at[0], e_rs.at[1], p.mate)
    value_side = c.astype(F32)
    finished = unrotate(
        kv_f32[c] + e1_recv[...].astype(F32) + e2_recv[...].astype(F32),
        cosine * (1.0 - value_side) + value_side,
        sine * (1.0 - value_side),
        sign,
    ).astype(BF16)
    rs_rows[pl.ds(0, ROWS), :] += 0.5 * finished.astype(F32) * kvraw[c]
    ones = jnp.ones((8, 128), F32)
    stat = jnp.concatenate([exact_nt(ones, rs_rows[0:128, :]), exact_nt(ones, rs_rows[128:256, :])], axis=0)
    coarse = stat.astype(BF16).astype(F32)
    ebuf[p.y, pl.ds(0, ROWS)] = finished
    ebuf[p.y, pl.ds(ROWS, 16)] = jnp.where(lax.rem(iota((16, 128), 0), 2) == 0, coarse, stat - coarse).astype(BF16)
    for k in (1, 2, 3):
        links.send(ebuf.at[p.y], ebuf.at[p.y], e_ss.at[1], e_rs.at[2], p.tid(p.ydst(k), p.x, c))
    f_mate(2)
    f_rest(2)
    f_relay_mate(3)
    f_relay_mirror(3)
    products(1)
    f_cores_far(1)
    f_cores_mate(1)
    f_cores_rest(1)
    f_far(1)
    f_relay_mate(2)
    f_relay_mirror(2)
    products(0)
    f_cores_far(0)
    f_cores_mate(0)
    f_mate(1)
    f_rest(1)
    f_third(3)
    f_relay_mate(1)
    f_relay_mirror(1)
    f_far(0)
    f_mate(0)
    links.wait(ebuf.at[pl.ds(0, 3)], e_ss.at[1], e_rs.at[2], p.partner)
    pair_grads = jnp.concatenate([ebuf[i, pl.ds(0, ROWS)] for i in range(4)], axis=1)
    (_, w_me), (_, w_partner), (_, w_mirror), (_, w_mirror_other) = weights_of
    f_core(0, mirror_shift, 8, mm_nt(pair_grads, w_mirror_other[...]))
    f_core(0, 0, 8, mm_nt(pair_grads, w_partner[...]))
    row_sum = jnp.zeros((16, 128), F32)
    for i in range(4):
        row_sum = row_sum + ebuf[i, pl.ds(ROWS, 16)].astype(F32)
    rs_all[p.row_index] = row_sum
    for j in range(1, 8):
        own_row = rs_all.at[p.row_index]
        links.send(own_row, own_row, e_ss.at[2], e_rs.at[3], p.in_row(j))
    mirror_part = mm_nt(pair_grads, w_mirror[...])
    own_part = mm_nt(pair_grads, w_me[...])
    f_rest(0, mirror_part, own_part)
    f_third(2)
    f_third(1)
    f_relay_mate(0)
    f_relay_mirror(0)
    links.wait(rs_all.at[pl.ds(0, 7)], e_ss.at[2], e_rs.at[3], p.partner)
    stats = rs_all[0]
    for j in range(1, 8):
        stats = stats + rs_all[j]
    eye = iota((128, 128), 0) == iota((128, 128), 1)

    def upright(row):
        return jnp.sum(jnp.where(eye, jnp.broadcast_to(row, (128, 128)), 0.0), axis=1, keepdims=True)

    row_stat = jnp.concatenate(
        [upright(stats[0:1] + stats[1:2]), upright(stats[8:9] + stats[9:10])[: ROWS - 128]], axis=0
    ) * (1.0 / D)
    f_third(0)
    normed_grad = s_own[0]
    for k in (1, 2):
        links.wait(y_recv.at[k], f_ss.at[2], f_rs.at[23 + k], p.tid(p.ysrc(k), p.x, c))
        normed_grad = normed_grad + y_recv[k].astype(F32)
    own_gain = jnp.concatenate([gain[pl.ds(2 * t, 1), :], gain[pl.ds(2 * t + 1, 1), :]], axis=1)
    grad[...] = (
        inverse * (own_gain * normed_grad)
        - jnp.concatenate([full_low[t], full_high[t]], axis=1).astype(F32) * (inverse * inverse * inverse * row_stat)
    ).astype(BF16)
    grad_copy = pltpu.make_async_copy(grad, grad_out, local_sem.at[14])
    grad_copy.start()
    most = a_send.at[:, pl.ds(0, N_DP - 1)]
    rollout(most, most, 0, lax.rem(dp + 1, N_DP)).wait_send()
    for tree in trees:
        tree.sent()
    links.sent(w_far, d_ss.at[0], d_rs.at[0], p.partner)
    links.sent(d2_send, d_ss.at[1], d_rs.at[1], p.mate)
    links.sent(kvraw.at[c], d_ss.at[2], d_rs.at[3], p.partner)
    links.sent(e1_send, e_ss.at[0], e_rs.at[0], p.partner)
    links.sent(ebuf.at[pl.ds(0, 3)], e_ss.at[1], e_rs.at[2], p.partner)
    links.sent(rs_all.at[pl.ds(0, 7)], e_ss.at[2], e_rs.at[3], p.partner)
    links.sent(f0_send, f_ss.at[0], f_rs.at[0], p.partner)
    links.sent(f0_send.at[pl.ds(0, 3)], f_ss.at[1], f_rs.at[0], p.partner)
    links.sent(y_send.at[pl.ds(0, 3)], f_ss.at[2], f_rs.at[0], p.partner)
    att_copy.wait()
    grad_copy.wait()


def hand_over(att_in, grad_in, att_out, grad_out):
    att_out[...] = att_in[...]
    grad_out[...] = grad_in[...]


def on_device(
    hidden_slots, lengths, owners, norm_gain, w_query, query_bias, w_keyvalue, keyvalue_bias, grad_attention
):
    frequency = ROPE_BASE ** (-2.0 * np.arange(HALF_DIM, dtype=np.float32) / HEAD_DIM)
    angles = np.arange(WINDOW, dtype=np.float32)[:, None] * frequency[None, :].astype(np.float32)
    angles = np.concatenate([angles, angles], axis=1)
    cosine = jnp.asarray(np.cos(angles), F32)
    sine = jnp.asarray(np.sin(angles), F32)
    operands = (
        hidden_slots, lengths, owners, norm_gain.reshape(64, 128), w_query, query_bias.reshape(2, 128),
        w_keyvalue, keyvalue_bias.reshape(16, 128), grad_attention, cosine, sine,
    )

    def v(*shape, dtype=BF16):
        return pltpu.VMEM(shape, dtype)

    def dma(n):
        return pltpu.SemaphoreType.DMA((n,))

    scratch = [pltpu.VMEM(one.shape, one.dtype) for i, one in enumerate(operands) if i != 6]
    scratch += [v(ROWS, PART), v(ROWS, PART)]
    scratch += [
        pltpu.SMEM((N_DP, N_DP), jnp.int32), v(2, N_DP, WINDOW, 128), v(2, N_DP, WINDOW, 128), v(LANES, ROWS, 128),
        v(LANES, ROWS, 128), v(ROWS, PART, dtype=F32),
        v(ROWS, 128, dtype=F32),
    ]
    scratch += [
        v(2, 2, PART, 512), v(3, PART, 512), v(4, ROWS, 128, dtype=F32),
        v(4, ROWS, 128), v(4, ROWS, 128), v(ROWS, 128), v(ROWS, 128), v(2, ROWS, 128, dtype=F32),
    ]
    scratch += [
        v(ROWS, 128, dtype=F32), v(ROWS, 128, dtype=F32), v(ROWS, PART), v(2, ROWS, 128, dtype=F32),
        v(2, ROWS, 128), v(ROWS, 128), v(ROWS, 128), v(ROWS, 128),
        v(4, GRAD_ROWS, 128), v(256, 128, dtype=F32), v(8, 16, 128, dtype=F32),
        v(4, ROWS, 8 * PART, dtype=F32),
    ]
    scratch += [
        v(4, 4, ROWS, PART), v(4, 4, ROWS, PART), v(4, ROWS, PART), v(4, HALF, PART), v(4, HALF, PART),
        v(4, ROWS, PART), v(4, ROWS, PART), v(4, 2, ROWS, PART), v(4, ROWS, PART, dtype=F32),
        v(4, ROWS, PART, dtype=F32), v(4, ROWS, PART, dtype=F32), v(4, ROWS, PART), v(4, ROWS, PART),
    ]
    scratch += [
        dma(15), dma(1), dma(2), dma(2), dma(2 * TREE_SLOTS), dma(3), dma(4), dma(3), dma(4), dma(3), dma(27),
    ]
    shape = jax.ShapeDtypeStruct((ROWS, PART), BF16)
    outs = pl.pallas_call(
        kernel,
        out_shape=(shape, shape),
        in_specs=[pl.BlockSpec(memory_space=pltpu.HBM)] * len(operands),
        out_specs=[pl.BlockSpec(memory_space=pl.ANY)] * 2,
        scratch_shapes=scratch,
        compiler_params=pltpu.CompilerParams(
            collective_id=0, has_side_effects=True, vmem_limit_bytes=60 * 1024 * 1024
        ),
        name="step",
    )(*operands)
    return pl.pallas_call(hand_over, out_shape=(shape, shape), name="hand_over")(*outs)


def solution(mesh):
    in_specs = (
        P("dp", None, "tensor"),
        P(),
        P(),
        P(),
        P(None, "tensor"),
        P("tensor"),
        P("tensor", None),
        P(),
        P("dp", "tensor"),
    )
    out_specs = (P("dp", "tensor"), P("dp", "tensor"))
    return jax.shard_map(on_device, mesh=mesh, in_specs=in_specs, out_specs=out_specs, check_vma=False)
```

time: 80.6 us -> 75.9 us (0.942)
  Pallas kernels: 79.5 us -> 75.1 us
    pallas_call x1, Pallas kernels: 77.9 us -> 73.5 us  [on_device(): pl.pallas_call(kernel, out_shape=(shape, shape), in_specs=[pl.BlockSpec(m...]
where the time goes in v3:
time: 75.9 us; the launch traced here: 75.8 us
  Pallas kernels  75.1 us (99%)
    pallas_call x1, Pallas kernels, on_device(): pl.pallas_call(kernel, out_shape=(shape, shape), in_specs=[pl.BlockSpec(m...  73.5 us
    pallas_call x1, Pallas kernels, on_device(): pl.pallas_call(hand_over, out_shape=(shape, shape), name='hand_over')(*outs)  1.62 us

profile of v3, /device:TPU:1, one launch (start us, length us, event | category | flops | bytes accessed | tf_op | source)
XLA Modules:
  0.0 75.8 jit_solution(18145666145200335167)
XLA Ops:
  0.6 73.5 %step.1 = (bf16[192,256]{1,0:T(8,128)(2,1)}, bf16[192,256]{1,0:T(8,128)(2,1)}) custom-call(bf16[24,16,256]{2,1,0:T(8,128)(2,1)} %slots_in.1, s32[24,24]{1,0:T(8,128)} %lengths_in.1, s32[24,24]{1,0:T(8,128)} %owners_in.1, f32[64,128]{1,0:T(8,128)} %bitcast.3, bf16[8192,256]{1,0:T(8,128)(2,1)} %wq_in.1, f32[2,128]{1,0:T(2,128)} %bitcast.5, ...), custom_call_target="tpu_custom_call" | custom-call | tf_op jit(solution)/shard_map/step/pallas_call | solution.py:690
  74.1 1.6 %hand_over.1 = (bf16[192,256]{1,0:T(8,128)(2,1)}, bf16[192,256]{1,0:T(8,128)(2,1)}) custom-call(bf16[192,256]{1,0:T(8,128)(2,1)} %get-tuple-element.4.att_in, bf16[192,256]{1,0:T(8,128)(2,1)} %get-tuple-element.5.grad_in), custom_call_target="tpu_custom_call" | custom-call | tf_op jit(solution)/shard_map/hand_over/pallas_call | solution.py:701

commit v4 on v3

--- a/solution.py
+++ b/solution.py
@@ -227,11 +227,12 @@
 
     barrier = pltpu.get_barrier_semaphore()
 
-    def greet(k, carry):
-        pl.semaphore_signal(barrier, inc=1, device_id=(lax.rem(dp + k, N_DP), t), device_id_type=MESH)
-        return carry
-
-    lax.fori_loop(1, N_DP, greet, 0)
+    half_index, depth = lax.div(dp, 12), lax.rem(dp, 12)
+    offsets = [(dh, dz) for dh in (0, 1) for dz in range(12) if dh or dz]
+    offsets.sort(key=lambda o: -(4 * o[0] + min(o[1], 12 - o[1])))
+    batch_peers = [lax.rem(half_index + dh, 2) * 12 + lax.rem(depth + dz, 12) for dh, dz in offsets]
+    for peer in batch_peers:
+        pl.semaphore_signal(barrier, inc=1, device_id=(peer, t), device_id_type=MESH)
     for peer in tuple(p.in_row(j) for j in range(1, 8)) + tuple(p.tid(p.ydst(k), p.x, c) for k in (1, 2, 3)):
         pl.semaphore_signal(barrier, inc=1, device_id=(dp, peer), device_id_type=MESH)
 
@@ -260,17 +261,13 @@
             src_ref=src, dst_ref=dst, send_sem=a_ss.at[0], recv_sem=a_rs.at[k], device_id=(peer, t), device_id_type=MESH
         )
 
-    def send_rollout(i, carry):
-        h, k = lax.div(i, N_DP - 1), lax.rem(i, N_DP - 1) + 1
-        peer = lax.rem(dp + k, N_DP)
-        rollout(a_send.at[h, peer], a_recv.at[h, dp], h, peer).start()
-        return carry
-
     def wait_rollout(h):
         most = a_recv.at[h, pl.ds(0, N_DP - 1)]
         rollout(most, most, h, lax.rem(dp + 1, N_DP)).wait_recv()
 
-    lax.fori_loop(0, 2 * (N_DP - 1), send_rollout, 0)
+    for h in (0, 1):
+        for peer in batch_peers:
+            rollout(a_send.at[h, peer], a_recv.at[h, dp], h, peer).start()
 
     pltpu.make_async_copy(w_own, w_own, local_sem.at[12]).wait()
     for one in loads[2:]:
@@ -508,8 +505,11 @@
             peer = p.tid(p.ydst(2 if k == 2 else 1), p.x, c)
             links.send(y_send.at[k], y_recv.at[k], f_ss.at[2], f_rs.at[23 + k], peer)
 
+    far_tid = p.tid(p.ydst(3), p.xat(2), 1 - c)
+    far_rows = pl.ds(pl.multiple_of(far_tid * PART, PART), PART)
+    f0_send[3, 2] = mm_nt(q_grad[...], wq[far_rows, :]).astype(BF16)
+    links.send(f0_send.at[3, 2], f0_recv.at[3, 2], f_ss.at[0], f_rs.at[3], p.partner)
     products(3)
-    f_cores_far(3)
     kv_f32[0] = mm_tn(score_grad, query)
     kv_f32[1] = mm_tn(low, upstream)
     e1_send[...] = kv_f32[...].astype(BF16)
@@ -540,6 +540,10 @@
     f_cores_rest(2)
     f_rest(3)
     f_far(2)
+    f_mate(2)
+    f_rest(2)
+    f_relay_mate(3)
+    f_relay_mirror(3)
     links.wait(e2_recv, e_ss.at[0], e_rs.at[1], p.mate)
     value_side = c.astype(F32)
     finished = unrotate(
@@ -556,10 +560,6 @@
     ebuf[p.y, pl.ds(ROWS, 16)] = jnp.where(lax.rem(iota((16, 128), 0), 2) == 0, coarse, stat - coarse).astype(BF16)
     for k in (1, 2, 3):
         links.send(ebuf.at[p.y], ebuf.at[p.y], e_ss.at[1], e_rs.at[2], p.tid(p.ydst(k), p.x, c))
-    f_mate(2)
-    f_rest(2)
-    f_relay_mate(3)
-    f_relay_mirror(3)
     products(1)
     f_cores_far(1)
     f_cores_mate(1)
@@ -637,9 +637,17 @@
     grad_copy.wait()
 
 
-def hand_over(att_in, grad_in, att_out, grad_out):
-    att_out[...] = att_in[...]
-    grad_out[...] = grad_in[...]
+def hand_over(att_in, grad_in, att_out, grad_out, att, grad, sems):
+    pairs = ((att_in, att, att_out), (grad_in, grad, grad_out))
+    inward = [pltpu.make_async_copy(a, b, sems.at[i]) for i, (a, b, _) in enumerate(pairs)]
+    outward = [pltpu.make_async_copy(b, o, sems.at[2 + i]) for i, (_, b, o) in enumerate(pairs)]
+    for one in inward:
+        one.start()
+    for one, two in zip(inward, outward):
+        one.wait()
+        two.start()
+    for two in outward:
+        two.wait()
 
 
 def on_device(
@@ -698,7 +706,16 @@
         ),
         name="step",
     )(*operands)
-    return pl.pallas_call(hand_over, out_shape=(shape, shape), name="hand_over")(*outs)
+    anywhere = [pl.BlockSpec(memory_space=pltpu.HBM)] * 2
+    return pl.pallas_call(
+        hand_over,
+        out_shape=(shape, shape),
+        in_specs=anywhere,
+        out_specs=anywhere,
+        scratch_shapes=[v(ROWS, PART), v(ROWS, PART), dma(4)],
+        compiler_params=pltpu.CompilerParams(vmem_limit_bytes=60 * 1024 * 1024),
+        name="hand_over",
+    )(*outs)
 
 
 def solution(mesh):

time: 75.9 us -> 76 us (level)
  no operation moved by 1% of the time
where the time goes in v4:
time: 76 us; the launch traced here: 75.8 us
  Pallas kernels  75.2 us (99%)
    pallas_call x1, Pallas kernels, on_device(): pl.pallas_call(kernel, out_shape=(shape, shape), in_specs=[pl.BlockSpec(m...  73.6 us
    pallas_call x1, Pallas kernels, on_device(): pl.pallas_call(hand_over, out_shape=(shape, shape), in_specs=anywhere, ou...  1.61 us

profile of v4, /device:TPU:1, one launch (start us, length us, event | category | flops | bytes accessed | tf_op | source)
XLA Modules:
  0.0 75.8 jit_solution(5744892662008479226)
XLA Ops:
  0.6 73.6 %step.1 = (bf16[192,256]{1,0:T(8,128)(2,1)}, bf16[192,256]{1,0:T(8,128)(2,1)}) custom-call(bf16[24,16,256]{2,1,0:T(8,128)(2,1)} %slots_in.1, s32[24,24]{1,0:T(8,128)} %lengths_in.1, s32[24,24]{1,0:T(8,128)} %owners_in.1, f32[64,128]{1,0:T(8,128)} %bitcast.3, bf16[8192,256]{1,0:T(8,128)(2,1)} %wq_in.1, f32[2,128]{1,0:T(2,128)} %bitcast.5, ...), custom_call_target="tpu_custom_call" | custom-call | tf_op jit(solution)/shard_map/step/pallas_call | solution.py:698
  74.2 1.6 %hand_over.1 = (bf16[192,256]{1,0:T(8,128)(2,1)}, bf16[192,256]{1,0:T(8,128)(2,1)}) custom-call(bf16[192,256]{1,0:T(8,128)(2,1)} %get-tuple-element.4.att_in, bf16[192,256]{1,0:T(8,128)(2,1)} %get-tuple-element.5.grad_in), custom_call_target="tpu_custom_call" | custom-call | tf_op jit(solution)/shard_map/hand_over/pallas_call | solution.py:710

commit v5 on v4

--- a/solution.py
+++ b/solution.py
@@ -297,7 +297,7 @@
     acc[...] = jnp.zeros_like(acc)
     ssq[...] = jnp.zeros_like(ssq)
     trees = [
-        Tree(links, p, ref, (80, 112), b_ss.at[h], b_rs, h * TREE_SLOTS) for h, ref in enumerate((full_low, full_high))
+        Tree(links, p, ref, (96, 96), b_ss.at[h], b_rs, h * TREE_SLOTS) for h, ref in enumerate((full_low, full_high))
     ]
     for h, ref in enumerate((full_low, full_high)):
         wait_rollout(h)
@@ -387,9 +387,9 @@
     steps("partner_near", 3)
     steps("partner_far", 1)
     steps("partner_far", 2)
-    consume((1 - c, 3, near), (1 - c, 1, far))
+    consume((1 - c, 3, near), (1 - c, 1, far), (1 - c, 2, far))
     steps("partner_far", 3)
-    consume((1 - c, 2, far), (1 - c, 3, far))
+    consume((1 - c, 3, far))
     links.wait(kvraw.at[1 - c], d_ss.at[2], d_rs.at[3], p.partner)
 
     cosine, sine = cos_s[...], sin_s[...]
@@ -413,7 +413,7 @@
     scores = jnp.where(both, mm_nt(query, key) * SCALE, -1e30)
     highest = jnp.max(scores, axis=1, keepdims=True)
     exponent = jnp.where(both, jnp.exp(scores - highest), 0.0)
-    weights = exponent / jnp.sum(exponent, axis=1, keepdims=True)
+    weights = exponent * (1.0 / jnp.sum(exponent, axis=1, keepdims=True))
     low = weights.astype(BF16)
     weight_grad = mm_nt(upstream, value)
     inner = jnp.sum(weights * weight_grad, axis=1, keepdims=True)
@@ -596,6 +596,7 @@
     f_third(1)
     f_relay_mate(0)
     f_relay_mirror(0)
+    f_third(0)
     links.wait(rs_all.at[pl.ds(0, 7)], e_ss.at[2], e_rs.at[3], p.partner)
     stats = rs_all[0]
     for j in range(1, 8):
@@ -608,7 +609,6 @@
     row_stat = jnp.concatenate(
         [upright(stats[0:1] + stats[1:2]), upright(stats[8:9] + stats[9:10])[: ROWS - 128]], axis=0
     ) * (1.0 / D)
-    f_third(0)
     normed_grad = s_own[0]
     for k in (1, 2):
         links.wait(y_recv.at[k], f_ss.at[2], f_rs.at[23 + k], p.tid(p.ysrc(k), p.x, c))

time: 76 us -> 76.1 us (level)
  no operation moved by 1% of the time
where the time goes in v5:
time: 76.1 us; the launch traced here: 75.9 us
  Pallas kernels  75.2 us (99%)
    pallas_call x1, Pallas kernels, on_device(): pl.pallas_call(kernel, out_shape=(shape, shape), in_specs=[pl.BlockSpec(m...  73.6 us
    pallas_call x1, Pallas kernels, on_device(): pl.pallas_call(hand_over, out_shape=(shape, shape), in_specs=anywhere, ou...  1.61 us

profile of v5, /device:TPU:1, one launch (start us, length us, event | category | flops | bytes accessed | tf_op | source)
XLA Modules:
  0.0 75.9 jit_solution(13884191864059802907)
XLA Ops:
  0.6 73.6 %step.1 = (bf16[192,256]{1,0:T(8,128)(2,1)}, bf16[192,256]{1,0:T(8,128)(2,1)}) custom-call(bf16[24,16,256]{2,1,0:T(8,128)(2,1)} %slots_in.1, s32[24,24]{1,0:T(8,128)} %lengths_in.1, s32[24,24]{1,0:T(8,128)} %owners_in.1, f32[64,128]{1,0:T(8,128)} %bitcast.3, bf16[8192,256]{1,0:T(8,128)(2,1)} %wq_in.1, f32[2,128]{1,0:T(2,128)} %bitcast.5, ...), custom_call_target="tpu_custom_call" | custom-call | tf_op jit(solution)/shard_map/step/pallas_call | solution.py:698
  74.3 1.6 %hand_over.1 = (bf16[192,256]{1,0:T(8,128)(2,1)}, bf16[192,256]{1,0:T(8,128)(2,1)}) custom-call(bf16[192,256]{1,0:T(8,128)(2,1)} %get-tuple-element.4.att_in, bf16[192,256]{1,0:T(8,128)(2,1)} %get-tuple-element.5.grad_in), custom_call_target="tpu_custom_call" | custom-call | tf_op jit(solution)/shard_map/hand_over/pallas_call | solution.py:710
